TPU v7x, 256 devices: a whole 4x4x8 slice. The times are simulated.
256 devices in a mesh: vert: 64 (over x, z, core), af: 4 (over y).
Axes of the slice: x: 4, y: 4, z: 8, core: 2. Of those that a mesh axis runs over, the one named last changes fastest.
Arguments:
- features_t: bfloat16 [128, 32768], P('af', 'vert'), may hold values from -24 to 24
- weight: bfloat16 [128, 256], P('af'), may hold values from -1 to 1
- bias: float32 [256], P('af'), may hold values from -3 to 3
- self_mask: int32 [64, 512, 512], P('vert'), may hold values 0 or 1
- halo_mask: int32 [64, 6, 512, 256], P('vert'), may hold values 0 or 1
- block_src: int32 [64, 6], P('vert'), may hold values from -1 to 63, as said below
- halo_rows: int32 [64, 6, 256], P('vert'), may hold values from 0 to 511, as said below
- outside_degree: int32 [32768], P('vert'), may hold values from 0 to 47
Outputs:
- output_t: bfloat16 [256, 32768], P('af', 'vert')
Inputs may be any that keep to these rules, and one draw needn't show every extreme that they name: `block_src`: the live sources of a row are distinct partitions other than the row's own; empty slots (-1) come after the live ones; every row has at least one live slot and some row has all 6. `halo_rows`: the entries of one slot are distinct.
All inputs are finite; a program needn't handle non-finite values. No bound on the sum of `self_mask` or of `halo_mask` on one device may be relied on, other than what follows from the above.
Results may differ from a plain program's by a relative error of at most 0.0054.
Values may be sent and summed in bfloat16 or wider, within the bound.
No kernel may reach another device: no remote copies, remote signals or barrier semaphores. Data moves between devices by JAX's collectives and lax.ppermute only.
A program may use at most 64 MiB of HBM per device.

v0:
```python
import jax
import jax.numpy as jnp
from jax import lax
from jax.experimental import pallas as pl
from jax.experimental.pallas import tpu as pltpu
from jax.sharding import Mesh
from jax.sharding import PartitionSpec as P


VERT = ("x", "z", "core")
LANES = 128
FEATS = 32
VMEM = pltpu.VMEM
CHUNKS = 4
ROWS = 512 // CHUNKS


def shifted(array, axis, by):
    count = lax.axis_size(axis)
    return lax.ppermute(array, axis, [(i, (i + by) % count) for i in range(count)])


def opposed(array, by):
    count = lax.axis_size("z")
    pairs = [(2 * z + c, 2 * ((z + (by, -by)[c]) % count) + c) for z in range(count) for c in range(2)]
    return lax.ppermute(array, ("z", "core"), pairs)


def whole(count=1):
    return [pl.BlockSpec(memory_space=VMEM)] * count


def in_hbm(array):
    return pltpu.with_memory_space_constraint(array, pltpu.HBM)


def head_kernel(
    sources_in, self_in, halo_in, outside_in, features_in, rows_in,
    scaled, root, request,
    sources, self_mask, halo_mask, outside, features, rows, small, large,
):
    smalls = [
        pltpu.make_async_copy(src, dst, small.at[k])
        for k, (src, dst) in enumerate(
            (
                (sources_in, sources),
                (outside_in, outside),
                (features_in, features),
                (rows_in, rows),
            )
        )
    ]
    larges = []
    for r in range(CHUNKS):
        at = pl.ds(r * ROWS, ROWS)
        larges.append(pltpu.make_async_copy(halo_in.at[0, :, at, :], halo_mask.at[:, at, :], large.at[r, 0]))
        larges.append(pltpu.make_async_copy(self_in.at[0, at, :], self_mask.at[at, :], large.at[r, 1]))
    smalls[0].start()
    for copy in larges[:2] + smalls[1:] + larges[2:]:
        copy.start()
    for copy in smalls:
        copy.wait()

    for s in range(6):
        for g in range(2):
            request[s : s + 1, g * LANES : (g + 1) * LANES] = rows[2 * s + g]
    lane = lax.broadcasted_iota(jnp.int32, (2, 256), 1)
    listed = jnp.full((2, 256), -1, jnp.int32)
    for s in range(6):
        listed = jnp.where(lane == s, sources[0, s], listed)
    request[6:8, :] = listed

    ones = jnp.ones((8, LANES), jnp.bfloat16)
    live = [(sources[0, s] >= 0).astype(jnp.int32) for s in range(6)]
    for r in range(CHUNKS):
        larges[2 * r].wait()
        larges[2 * r + 1].wait()
        at = slice(r * ROWS, (r + 1) * ROWS)
        total = self_mask[at, :LANES]
        for t in range(1, 4):
            total = total + self_mask[at, t * LANES : (t + 1) * LANES]
        for s in range(6):
            total = total + (halo_mask[s, at, :LANES] + halo_mask[s, at, LANES:]) * live[s]
        counts = total.astype(jnp.float32).astype(jnp.bfloat16)
        summed = lax.dot_general(ones, counts, (((1,), (1,)), ((), ())), preferred_element_type=jnp.float32)
        degree = summed[:1] + 1.0 + outside[:, at].astype(jnp.float32)
        inverse = 1.0 / jnp.sqrt(degree)
        root[:, at] = inverse
        scaled[:, at] = (features[:, at].astype(jnp.float32) * inverse).astype(jnp.bfloat16)


def head(block_src, self_mask, halo_mask, outside_degree, features_t, halo_rows):
    return pl.pallas_call(
        head_kernel,
        out_shape=[
            pltpu.VMEM((FEATS, 512), jnp.bfloat16),
            pltpu.VMEM((1, 512), jnp.float32),
            pltpu.VMEM((8, 256), jnp.int32),
        ],
        in_specs=[pl.BlockSpec(memory_space=pltpu.HBM)] * 6,
        out_specs=whole(3),
        scratch_shapes=[
            pltpu.SMEM((1, 6), jnp.int32),
            VMEM((512, 512), jnp.int32),
            VMEM((6, 512, 256), jnp.int32),
            VMEM((1, 512), jnp.int32),
            VMEM((FEATS, 512), jnp.bfloat16),
            VMEM((12, 1, LANES), jnp.int32),
            pltpu.SemaphoreType.DMA((4,)),
            pltpu.SemaphoreType.DMA((CHUNKS, 2)),
        ],
        compiler_params=pltpu.CompilerParams(vmem_limit_bytes=8 * 2**20),
        name="head",
    )(
        *map(
            in_hbm,
            (
                block_src,
                self_mask,
                halo_mask,
                outside_degree.reshape(1, 512),
                features_t,
                halo_rows.reshape(12, 1, LANES),
            ),
        )
    )


def select_kernel(table, *refs):
    requests, pieces, outs, held = refs[:4], refs[4:-5], refs[-5:-1], refs[-1]
    first = 0
    for piece in pieces:
        for k in range(piece.shape[0] // FEATS):
            held[first] = piece[k * FEATS : (k + 1) * FEATS, :].astype(jnp.float32)
            first += 1
    for k in range(4):
        outs[k][...] = jnp.zeros_like(outs[k])
        for s in range(6):
            which = table[k * 256 + s]

            @pl.when(which >= 0)
            def _():
                for g in range(2):
                    rows = requests[k][s : s + 1, g * LANES : (g + 1) * LANES]
                    rows = jnp.broadcast_to(rows, (FEATS, LANES))
                    lane = rows & (LANES - 1)
                    block = rows >> 7
                    picked = jnp.zeros((FEATS, LANES), jnp.float32)
                    for t in range(4):
                        part = held[which, :, t * LANES : (t + 1) * LANES]
                        took = jnp.take_along_axis(part, lane, axis=1, mode="promise_in_bounds")
                        picked = jnp.where(block == t, took, picked)
                    at = s * 256 + g * LANES
                    outs[k][:, at : at + LANES] = picked.astype(jnp.bfloat16)


def selected(table, requests, pieces):
    return pl.pallas_call(
        select_kernel,
        out_shape=[pltpu.VMEM((FEATS, 1536), jnp.bfloat16)] * 4,
        in_specs=[pl.BlockSpec(memory_space=pltpu.SMEM)] + whole(4 + len(pieces)),
        out_specs=whole(4),
        scratch_shapes=[pltpu.VMEM((16, FEATS, 512), jnp.float32)],
        compiler_params=pltpu.CompilerParams(vmem_limit_bytes=8 * 2**20),
        name="select",
    )(table, *requests, *pieces)


def prepare_kernel(halo_mask, turned):
    turned[...] = halo_mask[0, 0].astype(jnp.float32).T.astype(jnp.bfloat16)


def prepared(halo_mask):
    return pl.pallas_call(
        prepare_kernel,
        grid=(6,),
        out_shape=pltpu.VMEM((1536, 512), jnp.bfloat16),
        in_specs=[pl.BlockSpec((1, 1, 512, 256), lambda s: (0, s, 0, 0))],
        out_specs=pl.BlockSpec((256, 512), lambda s: (s, 0)),
        compiler_params=pltpu.CompilerParams(vmem_limit_bytes=8 * 2**20),
        name="prepare",
    )(in_hbm(halo_mask))


def aggregate_kernel(mine, one, two, three, turned, begun, root, columns, *outs):
    halo_vals = mine[...] + one[...] + two[...] + three[...]
    summed = begun[...] + jnp.dot(halo_vals, turned[...], preferred_element_type=jnp.float32)
    aggregated = (summed * root[...]).astype(jnp.bfloat16)
    for k in range(4):
        outs[k][:, :512] = aggregated
        outs[k][:, 512:] = columns[k]


def aggregate(vals, turned, begun, root, columns):
    return pl.pallas_call(
        aggregate_kernel,
        out_shape=[pltpu.VMEM((FEATS, 640), jnp.bfloat16)] * 4,
        in_specs=whole(8),
        out_specs=whole(4),
        compiler_params=pltpu.CompilerParams(vmem_limit_bytes=8 * 2**20),
        name="aggregate",
    )(*vals, turned, begun, root, columns)


def mix_kernel(*refs):
    parts, bias, out = refs[:4], refs[4], refs[5]
    mixed = jnp.broadcast_to(bias[...], (64, 512))
    for part in parts:
        mixed = mixed + lax.dot_general(
            part[:, 512 : 512 + 64], part[:, :512], (((0,), (0,)), ((), ())), preferred_element_type=jnp.float32
        )
    out[...] = jnp.maximum(mixed, 0.0).astype(jnp.bfloat16)


def mix(parts, bias):
    return pl.pallas_call(
        mix_kernel,
        out_shape=jax.ShapeDtypeStruct((64, 512), jnp.bfloat16),
        in_specs=whole(5),
        out_specs=whole(1)[0],
        compiler_params=pltpu.CompilerParams(vmem_limit_bytes=8 * 2**20),
        name="mix",
    )(*parts, bias.reshape(64, 1))


def piece_table(requests):
    my_x, my_z, my_core = (lax.axis_index(a) for a in VERT)
    wanted = jnp.concatenate([r[6] for r in requests])
    ahead = (wanted >> 1) - my_z
    ahead = jnp.where(my_core == 0, -ahead, ahead) & 7
    same = (wanted & 1) == my_core
    place = jnp.zeros_like(wanted)
    for distance, (ours, theirs) in enumerate(
        ((0, 1), (4, 5), (2, 3), (6, 7), (8, 15), (14, 13), (10, 9), (12, 11))
    ):
        place = jnp.where(ahead == distance, jnp.where(same, ours, theirs), place)
    here = (wanted >= 0) & ((wanted >> 4) == my_x)
    return jnp.where(here, place, -1)


def body(features_t, weight, bias, self_mask, halo_mask, block_src, halo_rows, outside_degree):
    scaled, root, request = head(block_src, self_mask, halo_mask, outside_degree, features_t, halo_rows)

    partner = shifted(scaled, "core", 1)
    both = jnp.concatenate([scaled, partner], axis=0)
    two = opposed(both, 2)
    four = shifted(scaled, "z", 4)
    one = opposed(jnp.concatenate([both, two], axis=0), 1)
    requests = [request]
    for k in (1, 2, 3):
        requests.append(shifted(request, "x", -k))
    table = piece_table(requests)
    rest = []
    for piece in (two, one, four):
        rest.append(shifted(piece, "core", 1))
    picked = selected(table, requests, (scaled, partner, two, one, four, *rest))
    vals = [picked[0]]
    for k in (1, 2, 3):
        vals.append(shifted(picked[k], "x", k))

    late_halo, late_self, _ = lax.optimization_barrier((halo_mask, self_mask, picked[0]))
    turned = prepared(late_halo)
    begun = scaled.astype(jnp.float32) + lax.dot_general(
        scaled, late_self[0].astype(jnp.bfloat16), (((1,), (1,)), ((), ())), preferred_element_type=jnp.float32
    )
    my_af = lax.axis_index("af")
    columns = jnp.stack(
        [
            jnp.pad(lax.dynamic_slice_in_dim(weight, jnp.mod(my_af + k, 4) * 64, 64, 1), ((0, 0), (0, 64)))
            for k in range(4)
        ]
    )
    sent = aggregate(vals, turned, begun, root, columns)
    parts = [sent[0]]
    for k in (1, 2, 3):
        parts.append(shifted(sent[k], "af", k))
    return mix(parts, bias)


def solution(mesh):
    finer = Mesh(mesh.devices.reshape(4, 8, 2, 4), ("x", "z", "core", "af"))
    return jax.shard_map(
        body,
        mesh=finer,
        in_specs=(
            P("af", VERT),
            P("af", None),
            P("af"),
            P(VERT, None, None),
            P(VERT, None, None, None),
            P(VERT, None),
            P(VERT, None, None),
            P(VERT),
        ),
        out_specs=P("af", VERT),
        check_vma=False,
    )
```

profile of v0, /device:TPU:2, one launch (start us, length us, event | category | flops | bytes accessed | tf_op | source)
XLA Modules:
  0.0 49.7 jit_solution(9803809732142293202)
XLA Ops:
  0.0 0.0 copy-start
  0.0 0.0 copy-start.1
  0.0 2.9 %head.1 = (bf16[32,512]{1,0:T(8,128)(2,1)S(1)}, f32[1,512]{1,0:T(1,128)S(1)}, s32[8,256]{1,0:T(8,128)S(1)}) custom-call(s32[1,6]{1,0:T(1,128)} %sources_in.1, s32[1,512,512]{2,1,0:T(8,128)} %self_in.1, s32[1,6,512,256]{3,2,1,0:T(8,128)} %halo_mask, s32[1,512]{1,0:T(1,128)} %bitcast.24, bf16[32,512]{1,0:T(8,128)(2,1)} %features_in.1, s32[12,1,128]{2,1,0:T(1,128)} %bitcast.19), custom_call_target="tpu_custom_call" | custom-call | tf_op jit(solution)/shard_map/head/pallas_call | solution.py:93
  2.9 0.1 collective-permute-start.3
  3.0 2.3 %collective-permute-start = (s32[8,256]{1,0:T(8,128)S(1)}, s32[8,256]{1,0:T(8,128)S(1)}, u32[]{:S(2)}, u32[]{:S(2)}) collective-permute-start(s32[8,256]{1,0:T(8,128)S(1)} %get-tuple-element.18.refs_0_), channel_id=1, source_target_pairs={{0,192},{64,0},{128,64},{192,128},{1,193},{65,1},{129,65},{193,129... | collective-permute-start | bytes 24584 | tf_op jit(solution)/shard_map/ppermute | solution.py:20
  5.3 0.7 %collective-permute-start.1 = (s32[8,256]{1,0:T(8,128)S(1)}, s32[8,256]{1,0:T(8,128)S(1)}, u32[]{:S(2)}, u32[]{:S(2)}) collective-permute-start(s32[8,256]{1,0:T(8,128)S(1)} %get-tuple-element.18.refs_0_), channel_id=1, source_target_pairs={{0,128},{64,192},{128,0},{192,64},{1,129},{65,193},{129,1},{193,65... | collective-permute-start | bytes 24584 | tf_op jit(solution)/shard_map/ppermute | solution.py:20
  6.0 1.8 %collective-permute-start.2 = (s32[8,256]{1,0:T(8,128)S(1)}, s32[8,256]{1,0:T(8,128)S(1)}, u32[]{:S(2)}, u32[]{:S(2)}) collective-permute-start(s32[8,256]{1,0:T(8,128)S(1)} %get-tuple-element.18.refs_0_), channel_id=1, source_target_pairs={{0,64},{64,128},{128,192},{192,0},{1,65},{65,129},{129,193},{193,1... | collective-permute-start | bytes 24584 | tf_op jit(solution)/shard_map/ppermute | solution.py:20
  7.8 7.2 %collective-permute-start.6 = (bf16[32,512]{1,0:T(8,128)(2,1)S(1)}, bf16[32,512]{1,0:T(8,128)(2,1)S(1)}, u32[]{:S(2)}, u32[]{:S(2)}) collective-permute-start(bf16[32,512]{1,0:T(8,128)(2,1)S(1)} %get-tuple-element.19.refs_4_), channel_id=1, source_target_pairs={{0,32},{8,40},{16,48},{24,56},{32,0},{40,8},{48,16},{56,24},{1,33}... | collective-permute-start | bytes 98312 | tf_op jit(solution)/shard_map/ppermute | solution.py:20
  15.0 0.0 collective-permute-done.3.refs_5_
  15.0 1.5 %collective-permute-start.4 = (bf16[64,512]{1,0:T(8,128)(2,1)S(1)}, bf16[64,512]{1,0:T(8,128)(2,1)S(1)}, u32[]{:S(2)}, u32[]{:S(2)}) collective-permute-start(bf16[64,512]{1,0:T(8,128)(2,1)S(1)} %pad_maximum_fusion.1), channel_id=1, source_target_pairs={{0,16},{4,52},{8,24},{12,60},{16,32},{20,4},{24,40},{28,12},{32,48... | collective-permute-start | bytes 196616 | tf_op jit(solution)/shard_map/ppermute | solution.py:26
  16.6 0.0 copy-done.1
  16.6 0.1 constant_dynamic-slice_fusion.3
  16.7 4.9 %collective-permute-done.4.refs_6_ = bf16[64,512]{1,0:T(8,128)(2,1)S(1)} collective-permute-done((bf16[64,512]{1,0:T(8,128)(2,1)S(1)}, bf16[64,512]{1,0:T(8,128)(2,1)S(1)}, u32[]{:S(2)}, u32[]{:S(2)}) %collective-permute-start.4) | collective-permute-done | bytes 65568 | tf_op jit(solution)/shard_map/ppermute | solution.py:26
  21.6 1.7 %collective-permute-start.5 = (bf16[128,512]{1,0:T(8,128)(2,1)S(1)}, bf16[128,512]{1,0:T(8,128)(2,1)S(1)}, u32[]{:S(2)}, u32[]{:S(2)}) collective-permute-start(bf16[128,512]{1,0:T(8,128)(2,1)S(1)} %pad_maximum_fusion), channel_id=1, source_target_pairs={{0,8},{4,60},{8,16},{12,4},{16,24},{20,12},{24,32},{28,20},{32,40}... | collective-permute-start | bytes 393224 | tf_op jit(solution)/shard_map/ppermute | solution.py:26
  23.3 4.5 %collective-permute-done.5.refs_7_ = bf16[128,512]{1,0:T(8,128)(2,1)S(1)} collective-permute-done((bf16[128,512]{1,0:T(8,128)(2,1)S(1)}, bf16[128,512]{1,0:T(8,128)(2,1)S(1)}, u32[]{:S(2)}, u32[]{:S(2)}) %collective-permute-start.5) | collective-permute-done | bytes 131104 | tf_op jit(solution)/shard_map/ppermute | solution.py:26
  27.9 0.0 collective-permute-start.8
  27.9 0.0 collective-permute-done.refs_1_
  27.9 0.0 collective-permute-done.1.refs_2_
  27.9 0.0 collective-permute-done.2.refs_3_
  28.0 0.0 collective-permute-done.6.refs_8_
  28.0 0.6 %collective-permute-start.9 = (bf16[32,512]{1,0:T(8,128)(2,1)S(1)}, bf16[32,512]{1,0:T(8,128)(2,1)S(1)}, u32[]{:S(2)}, u32[]{:S(2)}) collective-permute-start(bf16[32,512]{1,0:T(8,128)(2,1)S(1)} %collective-permute-done.6.refs_8_), channel_id=1, source_target_pairs={{0,4},{4,0},{1,5},{5,1},{2,6},{6,2},{3,7},{7,3},{8,12},{12,8},{9,1... | collective-permute-start | bytes 98312 | tf_op jit(solution)/shard_map/ppermute | solution.py:20
  28.6 0.1 collective-permute-start.7
  28.7 0.7 %collective-permute-done.9.refs_11_ = bf16[32,512]{1,0:T(8,128)(2,1)S(1)} collective-permute-done((bf16[32,512]{1,0:T(8,128)(2,1)S(1)}, bf16[32,512]{1,0:T(8,128)(2,1)S(1)}, u32[]{:S(2)}, u32[]{:S(2)}) %collective-permute-start.9) | collective-permute-done | bytes 32800 | tf_op jit(solution)/shard_map/ppermute | solution.py:20
  29.4 0.4 collective-permute-done.7.refs_9_
  29.8 0.0 collective-permute-done.8.refs_10_
  29.8 1.1 %select.13 = (bf16[32,1536]{1,0:T(8,128)(2,1)S(1)}, bf16[32,1536]{1,0:T(8,128)(2,1)S(1)}, bf16[32,1536]{1,0:T(8,128)(2,1)S(1)}, bf16[32,1536]{1,0:T(8,128)(2,1)S(1)}) custom-call(s32[1024]{0:T(1024)S(1)} %select_select_fusion.table, s32[8,256]{1,0:T(8,128)S(1)} %get-tuple-element.18.refs_0_, s32[8,256]{1,0:T(8,128)S(1)} %collective-permute-done.refs_1_, ...), custom_call_target="tpu_custom_call" | custom-call | tf_op jit(solution)/shard_map/select/pallas_call | solution.py:158
  30.9 0.3 collective-permute-start.10
  31.3 2.0 %collective-permute-start.11 = (bf16[32,1536]{1,0:T(8,128)(2,1)S(1)}, bf16[32,1536]{1,0:T(8,128)(2,1)S(1)}, u32[]{:S(2)}, u32[]{:S(2)}) collective-permute-start(bf16[32,1536]{1,0:T(8,128)(2,1)S(1)} %get-tuple-element.22), channel_id=1, source_target_pairs={{0,128},{64,192},{128,0},{192,64},{1,129},{65,193},{129,1},{193,65... | collective-permute-start | bytes 294920 | tf_op jit(solution)/shard_map/ppermute | solution.py:20
  33.2 1.9 %collective-permute-start.12 = (bf16[32,1536]{1,0:T(8,128)(2,1)S(1)}, bf16[32,1536]{1,0:T(8,128)(2,1)S(1)}, u32[]{:S(2)}, u32[]{:S(2)}) collective-permute-start(bf16[32,1536]{1,0:T(8,128)(2,1)S(1)} %get-tuple-element.23), channel_id=1, source_target_pairs={{0,192},{64,0},{128,64},{192,128},{1,193},{65,1},{129,65},{193,129... | collective-permute-start | bytes 294920 | tf_op jit(solution)/shard_map/ppermute | solution.py:20
  35.1 0.0 copy-done
  35.1 0.3 convolution_add_fusion.begun
  35.4 0.0 copy-start.2
  35.4 3.8 %prepare.1.turned = bf16[1536,512]{1,0:T(8,128)(2,1)S(1)} custom-call(s32[1,6,512,256]{3,2,1,0:T(8,128)} %halo_mask), custom_call_target="tpu_custom_call" | custom-call | tf_op jit(solution)/shard_map/prepare/pallas_call | solution.py:174
  39.2 0.0 collective-permute-done.10.one
  39.3 0.0 collective-permute-done.11.two
  39.3 0.6 %collective-permute-done.12.three = bf16[32,1536]{1,0:T(8,128)(2,1)S(1)} collective-permute-done((bf16[32,1536]{1,0:T(8,128)(2,1)S(1)}, bf16[32,1536]{1,0:T(8,128)(2,1)S(1)}, u32[]{:S(2)}, u32[]{:S(2)}) %collective-permute-start.12) | collective-permute-done | bytes 98336 | tf_op jit(solution)/shard_map/ppermute | solution.py:20
  39.9 0.4 aggregate.1
  40.3 1.7 %collective-permute-start.13 = (bf16[32,640]{1,0:T(8,128)(2,1)S(1)}, bf16[32,640]{1,0:T(8,128)(2,1)S(1)}, u32[]{:S(2)}, u32[]{:S(2)}) collective-permute-start(bf16[32,640]{1,0:T(8,128)(2,1)S(1)} %get-tuple-element.28), channel_id=1, source_target_pairs={{0,1},{1,2},{2,3},{3,0},{4,5},{5,6},{6,7},{7,4},{8,9},{9,10},{10,1... | collective-permute-start | bytes 122888 | tf_op jit(solution)/shard_map/ppermute | solution.py:20
  41.9 2.9 %collective-permute-start.14 = (bf16[32,640]{1,0:T(8,128)(2,1)S(1)}, bf16[32,640]{1,0:T(8,128)(2,1)S(1)}, u32[]{:S(2)}, u32[]{:S(2)}) collective-permute-start(bf16[32,640]{1,0:T(8,128)(2,1)S(1)} %get-tuple-element.29), channel_id=1, source_target_pairs={{0,2},{1,3},{2,0},{3,1},{4,6},{5,7},{6,4},{7,5},{8,10},{9,11},{10,... | collective-permute-start | bytes 122888 | tf_op jit(solution)/shard_map/ppermute | solution.py:20
  44.8 1.3 %collective-permute-start.15 = (bf16[32,640]{1,0:T(8,128)(2,1)S(1)}, bf16[32,640]{1,0:T(8,128)(2,1)S(1)}, u32[]{:S(2)}, u32[]{:S(2)}) collective-permute-start(bf16[32,640]{1,0:T(8,128)(2,1)S(1)} %get-tuple-element.30), channel_id=1, source_target_pairs={{0,3},{1,0},{2,1},{3,2},{4,7},{5,4},{6,5},{7,6},{8,11},{9,8},{10,9... | collective-permute-start | bytes 122888 | tf_op jit(solution)/shard_map/ppermute | solution.py:20
  46.2 0.0 copy-done.2
  46.2 0.1 copy.9.refs_4_
  46.3 0.0 collective-permute-done.13.refs_1_
  46.3 1.2 %collective-permute-done.14.refs_2_ = bf16[32,640]{1,0:T(8,128)(2,1)S(1)} collective-permute-done((bf16[32,640]{1,0:T(8,128)(2,1)S(1)}, bf16[32,640]{1,0:T(8,128)(2,1)S(1)}, u32[]{:S(2)}, u32[]{:S(2)}) %collective-permute-start.14) | collective-permute-done | bytes 40992 | tf_op jit(solution)/shard_map/ppermute | solution.py:20
  47.4 1.4 %collective-permute-done.15.refs_3_ = bf16[32,640]{1,0:T(8,128)(2,1)S(1)} collective-permute-done((bf16[32,640]{1,0:T(8,128)(2,1)S(1)}, bf16[32,640]{1,0:T(8,128)(2,1)S(1)}, u32[]{:S(2)}, u32[]{:S(2)}) %collective-permute-start.15) | collective-permute-done | bytes 40992 | tf_op jit(solution)/shard_map/ppermute | solution.py:20
  48.8 0.9 %mix.1 = bf16[64,512]{1,0:T(8,128)(2,1)} custom-call(bf16[32,640]{1,0:T(8,128)(2,1)S(1)} %get-tuple-element.27.refs_0_, bf16[32,640]{1,0:T(8,128)(2,1)S(1)} %collective-permute-done.13.refs_1_, bf16[32,640]{1,0:T(8,128)(2,1)S(1)} %collective-permute-done.14.refs_2_, bf16[32,640]{1,0:T(8,128)(2,1)S(1)} %collective-permute-done.15.refs_3_, ...), custom_call_target="tpu_custom_call" | custom-call | tf_op jit(solution)/shard_map/mix/pallas_call | solution.py:216
  (10 shorter events, 0.1 us)
Async XLA Ops:
  0.0 35.1 %copy-start = (s32[1,512,512]{2,1,0:T(8,128)S(1)}, s32[1,512,512]{2,1,0:T(8,128)}, u32[]{:S(2)}) copy-start(s32[1,512,512]{2,1,0:T(8,128)} %self_in.1) | copy-start | bytes 3145732
  0.0 16.6 %copy-start.1 = (bf16[32,256]{1,0:T(8,128)(2,1)S(1)}, bf16[32,256]{1,0:T(8,128)(2,1)}, u32[]{:S(2)}) copy-start(bf16[32,256]{1,0:T(8,128)(2,1)} %param.9) | copy-start | bytes 49156
  2.9 12.1 %collective-permute-start.3 = (bf16[32,512]{1,0:T(8,128)(2,1)S(1)}, bf16[32,512]{1,0:T(8,128)(2,1)S(1)}, u32[]{:S(2)}, u32[]{:S(2)}) collective-permute-start(bf16[32,512]{1,0:T(8,128)(2,1)S(1)} %get-tuple-element.19.refs_4_), channel_id=1, source_target_pairs={{0,4},{4,0},{1,5},{5,1},{2,6},{6,2},{3,7},{7,3},{8,12},{12,8},{9,1... | collective-permute-start | bytes 98312 | tf_op jit(solution)/shard_map/ppermute | solution.py:20
  3.0 24.9 %collective-permute-start = (s32[8,256]{1,0:T(8,128)S(1)}, s32[8,256]{1,0:T(8,128)S(1)}, u32[]{:S(2)}, u32[]{:S(2)}) collective-permute-start(s32[8,256]{1,0:T(8,128)S(1)} %get-tuple-element.18.refs_0_), channel_id=1, source_target_pairs={{0,192},{64,0},{128,64},{192,128},{1,193},{65,1},{129,65},{193,129... | collective-permute-start | bytes 24584 | tf_op jit(solution)/shard_map/ppermute | solution.py:20
  5.3 22.6 %collective-permute-start.1 = (s32[8,256]{1,0:T(8,128)S(1)}, s32[8,256]{1,0:T(8,128)S(1)}, u32[]{:S(2)}, u32[]{:S(2)}) collective-permute-start(s32[8,256]{1,0:T(8,128)S(1)} %get-tuple-element.18.refs_0_), channel_id=1, source_target_pairs={{0,128},{64,192},{128,0},{192,64},{1,129},{65,193},{129,1},{193,65... | collective-permute-start | bytes 24584 | tf_op jit(solution)/shard_map/ppermute | solution.py:20
  6.0 21.9 %collective-permute-start.2 = (s32[8,256]{1,0:T(8,128)S(1)}, s32[8,256]{1,0:T(8,128)S(1)}, u32[]{:S(2)}, u32[]{:S(2)}) collective-permute-start(s32[8,256]{1,0:T(8,128)S(1)} %get-tuple-element.18.refs_0_), channel_id=1, source_target_pairs={{0,64},{64,128},{128,192},{192,0},{1,65},{65,129},{129,193},{193,1... | collective-permute-start | bytes 24584 | tf_op jit(solution)/shard_map/ppermute | solution.py:20
  7.8 20.1 %collective-permute-start.6 = (bf16[32,512]{1,0:T(8,128)(2,1)S(1)}, bf16[32,512]{1,0:T(8,128)(2,1)S(1)}, u32[]{:S(2)}, u32[]{:S(2)}) collective-permute-start(bf16[32,512]{1,0:T(8,128)(2,1)S(1)} %get-tuple-element.19.refs_4_), channel_id=1, source_target_pairs={{0,32},{8,40},{16,48},{24,56},{32,0},{40,8},{48,16},{56,24},{1,33}... | collective-permute-start | bytes 98312 | tf_op jit(solution)/shard_map/ppermute | solution.py:20
  15.0 6.6 %collective-permute-start.4 = (bf16[64,512]{1,0:T(8,128)(2,1)S(1)}, bf16[64,512]{1,0:T(8,128)(2,1)S(1)}, u32[]{:S(2)}, u32[]{:S(2)}) collective-permute-start(bf16[64,512]{1,0:T(8,128)(2,1)S(1)} %pad_maximum_fusion.1), channel_id=1, source_target_pairs={{0,16},{4,52},{8,24},{12,60},{16,32},{20,4},{24,40},{28,12},{32,48... | collective-permute-start | bytes 196616 | tf_op jit(solution)/shard_map/ppermute | solution.py:26
  21.6 6.3 %collective-permute-start.5 = (bf16[128,512]{1,0:T(8,128)(2,1)S(1)}, bf16[128,512]{1,0:T(8,128)(2,1)S(1)}, u32[]{:S(2)}, u32[]{:S(2)}) collective-permute-start(bf16[128,512]{1,0:T(8,128)(2,1)S(1)} %pad_maximum_fusion), channel_id=1, source_target_pairs={{0,8},{4,60},{8,16},{12,4},{16,24},{20,12},{24,32},{28,20},{32,40}... | collective-permute-start | bytes 393224 | tf_op jit(solution)/shard_map/ppermute | solution.py:26
  27.9 2.0 %collective-permute-start.8 = (bf16[128,512]{1,0:T(8,128)(2,1)S(1)}, bf16[128,512]{1,0:T(8,128)(2,1)S(1)}, u32[]{:S(2)}, u32[]{:S(2)}) collective-permute-start(bf16[128,512]{1,0:T(8,128)(2,1)S(1)} %collective-permute-done.5.refs_7_), channel_id=1, source_target_pairs={{0,4},{4,0},{1,5},{5,1},{2,6},{6,2},{3,7},{7,3},{8,12},{12,8},{9,1... | collective-permute-start | bytes 393224 | tf_op jit(solution)/shard_map/ppermute | solution.py:20
  28.0 1.4 %collective-permute-start.9 = (bf16[32,512]{1,0:T(8,128)(2,1)S(1)}, bf16[32,512]{1,0:T(8,128)(2,1)S(1)}, u32[]{:S(2)}, u32[]{:S(2)}) collective-permute-start(bf16[32,512]{1,0:T(8,128)(2,1)S(1)} %collective-permute-done.6.refs_8_), channel_id=1, source_target_pairs={{0,4},{4,0},{1,5},{5,1},{2,6},{6,2},{3,7},{7,3},{8,12},{12,8},{9,1... | collective-permute-start | bytes 98312 | tf_op jit(solution)/shard_map/ppermute | solution.py:20
  28.6 1.3 %collective-permute-start.7 = (bf16[64,512]{1,0:T(8,128)(2,1)S(1)}, bf16[64,512]{1,0:T(8,128)(2,1)S(1)}, u32[]{:S(2)}, u32[]{:S(2)}) collective-permute-start(bf16[64,512]{1,0:T(8,128)(2,1)S(1)} %collective-permute-done.4.refs_6_), channel_id=1, source_target_pairs={{0,4},{4,0},{1,5},{5,1},{2,6},{6,2},{3,7},{7,3},{8,12},{12,8},{9,1... | collective-permute-start | bytes 196616 | tf_op jit(solution)/shard_map/ppermute | solution.py:20
  30.9 8.3 %collective-permute-start.10 = (bf16[32,1536]{1,0:T(8,128)(2,1)S(1)}, bf16[32,1536]{1,0:T(8,128)(2,1)S(1)}, u32[]{:S(2)}, u32[]{:S(2)}) collective-permute-start(bf16[32,1536]{1,0:T(8,128)(2,1)S(1)} %get-tuple-element.21), channel_id=1, source_target_pairs={{0,64},{64,128},{128,192},{192,0},{1,65},{65,129},{129,193},{193,1... | collective-permute-start | bytes 294920 | tf_op jit(solution)/shard_map/ppermute | solution.py:20
  31.3 8.0 %collective-permute-start.11 = (bf16[32,1536]{1,0:T(8,128)(2,1)S(1)}, bf16[32,1536]{1,0:T(8,128)(2,1)S(1)}, u32[]{:S(2)}, u32[]{:S(2)}) collective-permute-start(bf16[32,1536]{1,0:T(8,128)(2,1)S(1)} %get-tuple-element.22), channel_id=1, source_target_pairs={{0,128},{64,192},{128,0},{192,64},{1,129},{65,193},{129,1},{193,65... | collective-permute-start | bytes 294920 | tf_op jit(solution)/shard_map/ppermute | solution.py:20
  33.2 6.6 %collective-permute-start.12 = (bf16[32,1536]{1,0:T(8,128)(2,1)S(1)}, bf16[32,1536]{1,0:T(8,128)(2,1)S(1)}, u32[]{:S(2)}, u32[]{:S(2)}) collective-permute-start(bf16[32,1536]{1,0:T(8,128)(2,1)S(1)} %get-tuple-element.23), channel_id=1, source_target_pairs={{0,192},{64,0},{128,64},{192,128},{1,193},{65,1},{129,65},{193,129... | collective-permute-start | bytes 294920 | tf_op jit(solution)/shard_map/ppermute | solution.py:20
  35.4 10.8 %copy-start.2 = (f32[64]{0:T(128)S(1)}, f32[64]{0:T(128)}, u32[]{:S(2)}) copy-start(f32[64]{0:T(128)} %param.10) | copy-start | bytes 772
  40.3 6.0 %collective-permute-start.13 = (bf16[32,640]{1,0:T(8,128)(2,1)S(1)}, bf16[32,640]{1,0:T(8,128)(2,1)S(1)}, u32[]{:S(2)}, u32[]{:S(2)}) collective-permute-start(bf16[32,640]{1,0:T(8,128)(2,1)S(1)} %get-tuple-element.28), channel_id=1, source_target_pairs={{0,1},{1,2},{2,3},{3,0},{4,5},{5,6},{6,7},{7,4},{8,9},{9,10},{10,1... | collective-permute-start | bytes 122888 | tf_op jit(solution)/shard_map/ppermute | solution.py:20
  41.9 5.5 %collective-permute-start.14 = (bf16[32,640]{1,0:T(8,128)(2,1)S(1)}, bf16[32,640]{1,0:T(8,128)(2,1)S(1)}, u32[]{:S(2)}, u32[]{:S(2)}) collective-permute-start(bf16[32,640]{1,0:T(8,128)(2,1)S(1)} %get-tuple-element.29), channel_id=1, source_target_pairs={{0,2},{1,3},{2,0},{3,1},{4,6},{5,7},{6,4},{7,5},{8,10},{9,11},{10,... | collective-permute-start | bytes 122888 | tf_op jit(solution)/shard_map/ppermute | solution.py:20
  44.8 4.0 %collective-permute-start.15 = (bf16[32,640]{1,0:T(8,128)(2,1)S(1)}, bf16[32,640]{1,0:T(8,128)(2,1)S(1)}, u32[]{:S(2)}, u32[]{:S(2)}) collective-permute-start(bf16[32,640]{1,0:T(8,128)(2,1)S(1)} %get-tuple-element.30), channel_id=1, source_target_pairs={{0,3},{1,0},{2,1},{3,2},{4,7},{5,4},{6,5},{7,6},{8,11},{9,8},{10,9... | collective-permute-start | bytes 122888 | tf_op jit(solution)/shard_map/ppermute | solution.py:20
where the time goes:
time: 49.9 us; the launch traced here: 49.7 us
  starting transfers between devices  26.1 us (52%)
  waiting for transfers between devices  13.8 us (28%)
  Pallas kernels  9.08 us (18%)
    ppermute x14, starting transfers between devices, shifted(): lax.ppermute(array, axis, [(i, (i + by) % count) for i in range(count)])  22.9 us
    ppermute x2, waiting for transfers between devices, opposed(): return lax.ppermute(array, ('z', 'core'), pairs)  9.46 us
    ppermute x14, waiting for transfers between devices, shifted(): lax.ppermute(array, axis, [(i, (i + by) % count) for i in range(count)])  4.32 us
    pallas_call x1, Pallas kernels, prepared(): pl.pallas_call(prepare_kernel, grid=(6,), out_shape=pltpu.VMEM((1536, 512...  3.81 us
    ppermute x2, starting transfers between devices, opposed(): return lax.ppermute(array, ('z', 'core'), pairs)  3.24 us
    pallas_call x1, Pallas kernels, head(): pl.pallas_call(head_kernel, out_shape=[pltpu.VMEM((FEATS, 512), jnp.bfloa...  2.89 us
    pallas_call x1, Pallas kernels, selected(): pl.pallas_call(select_kernel, out_shape=[pltpu.VMEM((FEATS, 1536), jnp.bf...  1.11 us
  transfers between devices with their start and end apart: 16, of which 7 were waited for; matrix products, arithmetic and copies ran while one was open for 1% of the time, Pallas kernels for 8%

commit v1 on v0

v1 whole, which is shorter than its diff:
```python
import jax
import jax.numpy as jnp
from jax import lax
from jax.experimental import pallas as pl
from jax.experimental.pallas import tpu as pltpu
from jax.sharding import Mesh
from jax.sharding import PartitionSpec as P


VERT = ("x", "z", "core")
LANES = 128
FEATS = 32
SURE = 3
VMEM = pltpu.VMEM


def shifted(array, axis, by):
    count = lax.axis_size(axis)
    return lax.ppermute(array, axis, [(i, (i + by) % count) for i in range(count)])


def paired(array, axis, by):
    return lax.ppermute(array, axis, [(i, i ^ by) for i in range(lax.axis_size(axis))])


def opposed(array, by):
    count = lax.axis_size("z")
    pairs = [(2 * z + c, 2 * ((z + (by, -by)[c]) % count) + c) for z in range(count) for c in range(2)]
    return lax.ppermute(array, ("z", "core"), pairs)


def whole(count=1):
    return [pl.BlockSpec(memory_space=VMEM)] * count


def in_hbm(array):
    return pltpu.with_memory_space_constraint(array, pltpu.HBM)


def head_kernel(
    sources_in, self_in, halo_in, outside_in, features_in, rows_in,
    scaled, root, request, self_out, halo_out,
    sources, self_mask, halo_mask, outside, features, rows, total, small, own, slot,
):
    smalls = [
        pltpu.make_async_copy(src, dst, small.at[k])
        for k, (src, dst) in enumerate(
            (
                (sources_in, sources),
                (outside_in, outside),
                (features_in, features),
                (rows_in, rows),
            )
        )
    ]
    owns = [
        pltpu.make_async_copy(
            self_in.at[0, pl.ds(r * 256, 256), :], self_mask.at[pl.ds(r * 256, 256), :], own.at[r]
        )
        for r in range(2)
    ]
    slots = [pltpu.make_async_copy(halo_in.at[0, s], halo_mask.at[s], slot.at[s]) for s in range(6)]
    smalls[0].start()
    owns[0].start()
    owns[1].start()
    for s in range(SURE):
        slots[s].start()
    for copy in smalls[1:]:
        copy.start()
    smalls[0].wait()
    for s in range(SURE, 6):
        pl.when(sources[0, s] >= 0)(slots[s].start)
    for copy in smalls[1:]:
        copy.wait()

    for s in range(6):
        for g in range(2):
            request[s : s + 1, g * LANES : (g + 1) * LANES] = rows[2 * s + g]
    lane = lax.broadcasted_iota(jnp.int32, (2, 256), 1)
    listed = jnp.full((2, 256), -1, jnp.int32)
    for s in range(6):
        listed = jnp.where(lane == s, sources[0, s], listed)
    request[6:8, :] = listed

    for r in range(2):
        owns[r].wait()
        at = slice(r * 256, (r + 1) * 256)
        block = self_mask[at, :]
        self_out[at, :] = block.astype(jnp.float32).astype(jnp.bfloat16)
        total[at, :] = (block[:, :128] + block[:, 128:256]) + (block[:, 256:384] + block[:, 384:])
    for s in range(6):

        if s < SURE:
            slots[s].wait()

        def counted(s=s):
            if s >= SURE:
                slots[s].wait()
            block = halo_mask[s]
            halo_out[s] = block.astype(jnp.float32).astype(jnp.bfloat16)
            total[...] += block[:, :LANES] + block[:, LANES:]

        def left_out(s=s):
            halo_out[s] = jnp.zeros_like(halo_out[s])

        if s:
            live = sources[0, s] >= 0
            pl.when(live)(counted)
            pl.when(jnp.logical_not(live))(left_out)
        else:
            counted()
    ones = jnp.ones((8, LANES), jnp.bfloat16)
    counts = total[...].astype(jnp.float32).astype(jnp.bfloat16)
    summed = lax.dot_general(ones, counts, (((1,), (1,)), ((), ())), preferred_element_type=jnp.float32)
    inverse = lax.rsqrt(summed[:1] + 1.0 + outside[...].astype(jnp.float32))
    root[...] = inverse
    scaled[...] = (features[...].astype(jnp.float32) * inverse).astype(jnp.bfloat16)


def head(block_src, self_mask, halo_mask, outside_degree, features_t, halo_rows):
    return pl.pallas_call(
        head_kernel,
        out_shape=[
            VMEM((FEATS, 512), jnp.bfloat16),
            VMEM((1, 512), jnp.float32),
            VMEM((8, 256), jnp.int32),
            VMEM((512, 512), jnp.bfloat16),
            VMEM((6, 512, 256), jnp.bfloat16),
        ],
        in_specs=[pl.BlockSpec(memory_space=pltpu.HBM)] * 6,
        out_specs=whole(5),
        scratch_shapes=[
            pltpu.SMEM((1, 6), jnp.int32),
            VMEM((512, 512), jnp.int32),
            VMEM((6, 512, 256), jnp.int32),
            VMEM((1, 512), jnp.int32),
            VMEM((FEATS, 512), jnp.bfloat16),
            VMEM((12, 1, LANES), jnp.int32),
            VMEM((512, LANES), jnp.int32),
            pltpu.SemaphoreType.DMA((4,)),
            pltpu.SemaphoreType.DMA((2,)),
            pltpu.SemaphoreType.DMA((6,)),
        ],
        compiler_params=pltpu.CompilerParams(vmem_limit_bytes=8 * 2**20),
        name="head",
    )(
        *map(
            in_hbm,
            (
                block_src,
                self_mask,
                halo_mask,
                outside_degree.reshape(1, 512),
                features_t,
                halo_rows.reshape(12, 1, LANES),
            ),
        )
    )


def select_kernel(listed, *refs):
    requests, pieces, outs, (held, table, arrived) = refs[:4], refs[4:-7], refs[-7:-3], refs[-3:]
    tables = pltpu.make_async_copy(listed, table, arrived)
    tables.start()
    at = 0
    for piece in pieces:
        for k in range(piece.shape[0] // FEATS):
            held[at] = piece[k * FEATS : (k + 1) * FEATS, :].astype(jnp.float32)
            at += 1
    for out in outs:
        out[...] = jnp.zeros_like(out)
    tables.wait()
    for k in range(4):
        for s in range(6):
            which = table[k, s]

            @pl.when(which >= 0)
            def _():
                for g in range(2):
                    rows = requests[k][s : s + 1, g * LANES : (g + 1) * LANES]
                    rows = jnp.broadcast_to(rows, (FEATS, LANES))
                    lane = rows & (LANES - 1)
                    block = rows >> 7
                    picked = jnp.zeros((FEATS, LANES), jnp.float32)
                    for t in range(4):
                        part = held[which, :, t * LANES : (t + 1) * LANES]
                        took = jnp.take_along_axis(part, lane, axis=1, mode="promise_in_bounds")
                        picked = jnp.where(block == t, took, picked)
                    to = s * 256 + g * LANES
                    outs[k][:, to : to + LANES] = picked.astype(jnp.bfloat16)


def selected(table, requests, pieces):
    operands = (table, *requests, *pieces)
    return pl.pallas_call(
        select_kernel,
        out_shape=[VMEM((FEATS, 1536), jnp.bfloat16)] * 4,
        in_specs=whole(len(operands)),
        out_specs=whole(4),
        scratch_shapes=[
            VMEM((16, FEATS, 512), jnp.float32),
            pltpu.SMEM((4, LANES), jnp.int32),
            pltpu.SemaphoreType.DMA,
        ],
        compiler_params=pltpu.CompilerParams(vmem_limit_bytes=8 * 2**20),
        name="select",
    )(*operands)


def join_kernel(*refs):
    at = 0
    for piece in refs[:-1]:
        refs[-1][at : at + piece.shape[0], :] = piece[...]
        at += piece.shape[0]


def joined(*pieces):
    return pl.pallas_call(
        join_kernel,
        out_shape=VMEM((sum(p.shape[0] for p in pieces), 512), jnp.bfloat16),
        in_specs=whole(len(pieces)),
        out_specs=whole()[0],
        compiler_params=pltpu.CompilerParams(vmem_limit_bytes=2 * 2**20),
        name="join",
    )(*pieces)


def prepare_kernel(halo_mask, self_mask, scaled, turned, begun):
    for s in range(6):
        turned[s * 256 : (s + 1) * 256, :] = halo_mask[s].T
    begun[...] = scaled[...].astype(jnp.float32) + lax.dot_general(
        scaled[...], self_mask[...], (((1,), (1,)), ((), ())), preferred_element_type=jnp.float32
    )


def prepared(halo_mask, self_mask, scaled):
    return pl.pallas_call(
        prepare_kernel,
        out_shape=[VMEM((1536, 512), jnp.bfloat16), VMEM((FEATS, 512), jnp.float32)],
        in_specs=whole(3),
        out_specs=whole(2),
        compiler_params=pltpu.CompilerParams(vmem_limit_bytes=16 * 2**20),
        name="prepare",
    )(halo_mask, self_mask, scaled)


def aggregate_kernel(mine, one, two, three, turned, begun, root, columns, *outs):
    halo_vals = mine[...] + one[...] + two[...] + three[...]
    summed = begun[...] + jnp.dot(halo_vals, turned[...], preferred_element_type=jnp.float32)
    aggregated = (summed * root[...]).astype(jnp.bfloat16)
    for k in range(4):
        outs[k][:, :512] = aggregated
        outs[k][:, 512:] = columns[k]


def aggregate(vals, turned, begun, root, columns):
    return pl.pallas_call(
        aggregate_kernel,
        out_shape=[VMEM((FEATS, 640), jnp.bfloat16)] * 4,
        in_specs=whole(8),
        out_specs=whole(4),
        compiler_params=pltpu.CompilerParams(vmem_limit_bytes=8 * 2**20),
        name="aggregate",
    )(*vals, turned, begun, root, columns)


def mix_kernel(*refs):
    parts, bias, out = refs[:4], refs[4], refs[5]
    mixed = jnp.broadcast_to(bias[...], (64, 512))
    for part in parts:
        mixed = mixed + lax.dot_general(
            part[:, 512 : 512 + 64], part[:, :512], (((0,), (0,)), ((), ())), preferred_element_type=jnp.float32
        )
    out[...] = jnp.maximum(mixed, 0.0).astype(jnp.bfloat16)


def mix(parts, bias):
    return pl.pallas_call(
        mix_kernel,
        out_shape=jax.ShapeDtypeStruct((64, 512), jnp.bfloat16),
        in_specs=whole(5),
        out_specs=whole(1)[0],
        compiler_params=pltpu.CompilerParams(vmem_limit_bytes=8 * 2**20),
        name="mix",
    )(*parts, bias.reshape(64, 1))


def piece_table(requests):
    my_x, my_z, my_core = (lax.axis_index(a) for a in VERT)
    wanted = jnp.concatenate([r[6:7, :LANES] for r in requests], axis=0)
    ahead = (wanted >> 1) - my_z
    ahead = jnp.where(my_core == 0, -ahead, ahead) & 7
    same = (wanted & 1) == my_core
    place = jnp.zeros_like(wanted)
    for distance, (ours, theirs) in enumerate(
        ((0, 1), (4, 5), (2, 3), (6, 7), (8, 15), (14, 13), (10, 9), (12, 11))
    ):
        place = jnp.where(ahead == distance, jnp.where(same, ours, theirs), place)
    here = (wanted >= 0) & ((wanted >> 4) == my_x)
    return jnp.where(here, place, -1)


def body(features_t, weight, bias, self_mask, halo_mask, block_src, halo_rows, outside_degree):
    scaled, root, request, held_self, held_halo = head(block_src, self_mask, halo_mask, outside_degree, features_t, halo_rows)

    partner = shifted(scaled, "core", 1)
    both = joined(scaled, partner)
    two = opposed(both, 2)
    turned, begun = prepared(held_halo, held_self, scaled)
    weight, bias, _ = lax.optimization_barrier((weight, bias, begun))
    four = shifted(scaled, "z", 4)
    one = opposed(joined(both, two), 1)
    requests = [request]
    for k in (1, 2, 3):
        requests.append(paired(request, "x", k))
    *requests, _ = lax.optimization_barrier((*requests, begun))
    table = piece_table(requests)
    rest = []
    for piece in (two, one, four):
        rest.append(shifted(piece, "core", 1))
    picked = selected(table, requests, (scaled, partner, two, one, four, *rest))
    vals = [picked[0]]
    for k in (1, 2, 3):
        vals.append(paired(picked[k], "x", k))

    my_af = lax.axis_index("af")
    columns = jnp.stack(
        [
            jnp.pad(lax.dynamic_slice_in_dim(weight, (my_af ^ k) * 64, 64, 1), ((0, 0), (0, 64)))
            for k in range(4)
        ]
    )
    sent = aggregate(vals, turned, begun, root, columns)
    parts = [sent[0]]
    for k in (1, 2, 3):
        parts.append(paired(sent[k], "af", k))
    return mix(parts, bias)


def solution(mesh):
    finer = Mesh(mesh.devices.reshape(4, 8, 2, 4), ("x", "z", "core", "af"))
    return jax.shard_map(
        body,
        mesh=finer,
        in_specs=(
            P("af", VERT),
            P("af", None),
            P("af"),
            P(VERT, None, None),
            P(VERT, None, None, None),
            P(VERT, None),
            P(VERT, None, None),
            P(VERT),
        ),
        out_specs=P("af", VERT),
        check_vma=False,
    )
```

time: 49.9 us -> 50.2 us (level)
  the two profiles are of different devices: /device:TPU:2 before, /device:TPU:32 now
where the time goes in v1:
time: 50.2 us; the launch traced here: 49.3 us
  starting transfers between devices  22.7 us (45%)
  waiting for transfers between devices  18.9 us (38%)
  Pallas kernels  5.37 us (11%)
  local copies, waits for them, and re-layouts  2.06 us (4%)
    ppermute x9, starting transfers between devices, paired(): lax.ppermute(array, axis, [(i, i ^ by) for i in range(lax.axis_size(axis))])  14.3 us
    ppermute x9, waiting for transfers between devices, paired(): lax.ppermute(array, axis, [(i, i ^ by) for i in range(lax.axis_size(axis))])  11.7 us
    ppermute x5, starting transfers between devices, shifted(): lax.ppermute(array, axis, [(i, (i + by) % count) for i in range(count)])  5.04 us
    ppermute x2, waiting for transfers between devices, opposed(): return lax.ppermute(array, ('z', 'core'), pairs)  4.83 us
    ppermute x2, starting transfers between devices, opposed(): return lax.ppermute(array, ('z', 'core'), pairs)  3.35 us
    pallas_call x1, Pallas kernels, head(): pl.pallas_call(head_kernel, out_shape=[VMEM((FEATS, 512), jnp.bfloat16),...  2.69 us
    ppermute x5, waiting for transfers between devices, shifted(): lax.ppermute(array, axis, [(i, (i + by) % count) for i in range(count)])  2.34 us
    unnamed x8, local copies, waits for them, and re-layouts  1.84 us
  transfers between devices with their start and end apart: 16, of which 9 were waited for; matrix products, arithmetic and copies ran while one was open for 1% of the time, Pallas kernels for 1%

profile of v1, /device:TPU:32, one launch (start us, length us, event | category | flops | bytes accessed | tf_op | source)
XLA Modules:
  0.0 49.3 jit_solution(10162838157469610167)
XLA Ops:
  0.0 2.7 %head.1 = (bf16[32,512]{1,0:T(8,128)(2,1)S(1)}, f32[1,512]{1,0:T(1,128)S(1)}, s32[8,256]{1,0:T(8,128)S(1)}, bf16[512,512]{1,0:T(8,128)(2,1)S(1)}, bf16[6,512,256]{2,1,0:T(8,128)(2,1)S(1)}) custom-call(s32[1,6]{1,0:T(1,128)} %sources_in.1, s32[1,512,512]{2,1,0:T(8,128)} %self_in.1, s32[1,6,512,256]{3,2,1,0:T(8,128)} %halo_in.1, s32[1,512]{1,0:T(1,128)} %bitcast.12, ...), custom_call_target="tpu_custom_call" | custom-call | tf_op jit(solution)/shard_map/head/pallas_call | solution.py:121
  2.7 0.0 copy-start
  2.7 0.8 %copy-done = bf16[512,512]{1,0:T(8,128)(2,1)} copy-done((bf16[512,512]{1,0:T(8,128)(2,1)}, bf16[512,512]{1,0:T(8,128)(2,1)S(1)}, u32[]{:S(2)}) %copy-start) | copy-done | bytes 524312
  3.5 0.0 copy-start.2
  3.5 0.0 collective-permute-start.3
  3.5 1.2 %collective-permute-done.3.refs_1_.refs_5_ = bf16[32,512]{1,0:T(8,128)(2,1)S(1)} collective-permute-done((bf16[32,512]{1,0:T(8,128)(2,1)S(1)}, bf16[32,512]{1,0:T(8,128)(2,1)S(1)}, u32[]{:S(2)}, u32[]{:S(2)}) %collective-permute-start.3) | collective-permute-done | bytes 32800 | tf_op jit(solution)/shard_map/ppermute | solution.py:19
  4.7 3.3 %collective-permute-start.4 = (bf16[64,512]{1,0:T(8,128)(2,1)S(1)}, bf16[64,512]{1,0:T(8,128)(2,1)S(1)}, u32[]{:S(2)}, u32[]{:S(2)}) collective-permute-start(bf16[64,512]{1,0:T(8,128)(2,1)S(1)} %join.2.refs_0_), channel_id=1, source_target_pairs={{0,16},{4,52},{8,24},{12,60},{16,32},{20,4},{24,40},{28,12},{32,48... | collective-permute-start | bytes 196616 | tf_op jit(solution)/shard_map/ppermute | solution.py:29
  8.0 1.4 %collective-permute-start = (s32[8,256]{1,0:T(8,128)S(1)}, s32[8,256]{1,0:T(8,128)S(1)}, u32[]{:S(2)}, u32[]{:S(2)}) collective-permute-start(s32[8,256]{1,0:T(8,128)S(1)} %get-tuple-element.31.refs_0_), channel_id=1, source_target_pairs={{0,64},{64,0},{128,192},{192,128},{1,65},{65,1},{129,193},{193,129... | collective-permute-start | bytes 24584 | tf_op jit(solution)/shard_map/ppermute | solution.py:23
  9.3 2.3 %collective-permute-start.1 = (s32[8,256]{1,0:T(8,128)S(1)}, s32[8,256]{1,0:T(8,128)S(1)}, u32[]{:S(2)}, u32[]{:S(2)}) collective-permute-start(s32[8,256]{1,0:T(8,128)S(1)} %get-tuple-element.31.refs_0_), channel_id=1, source_target_pairs={{0,128},{64,192},{128,0},{192,64},{1,129},{65,193},{129,1},{193,65... | collective-permute-start | bytes 24584 | tf_op jit(solution)/shard_map/ppermute | solution.py:23
  11.6 1.1 %collective-permute-start.2 = (s32[8,256]{1,0:T(8,128)S(1)}, s32[8,256]{1,0:T(8,128)S(1)}, u32[]{:S(2)}, u32[]{:S(2)}) collective-permute-start(s32[8,256]{1,0:T(8,128)S(1)} %get-tuple-element.31.refs_0_), channel_id=1, source_target_pairs={{0,192},{64,128},{128,64},{192,0},{1,193},{65,129},{129,65},{193,1... | collective-permute-start | bytes 24584 | tf_op jit(solution)/shard_map/ppermute | solution.py:23
  12.7 4.4 %collective-permute-start.6 = (bf16[32,512]{1,0:T(8,128)(2,1)S(1)}, bf16[32,512]{1,0:T(8,128)(2,1)S(1)}, u32[]{:S(2)}, u32[]{:S(2)}) collective-permute-start(bf16[32,512]{1,0:T(8,128)(2,1)S(1)} %get-tuple-element.29.scaled.refs_0_.refs_4_), channel_id=1, source_target_pairs={{0,32},{8,40},{16,48},{24,56},{32,0},{40,8},{48,16},{56,24},{1,33}... | collective-permute-start | bytes 98312 | tf_op jit(solution)/shard_map/ppermute | solution.py:19
  17.1 0.0 copy-start.1
  17.1 1.0 %copy-done.1 = bf16[512,512]{1,0:T(8,128)(2,1)S(1)} copy-done((bf16[512,512]{1,0:T(8,128)(2,1)S(1)}, bf16[512,512]{1,0:T(8,128)(2,1)}, u32[]{:S(2)}) %copy-start.1) | copy-done | bytes 524312
  18.1 0.5 prepare.1
  18.6 0.0 copy-start.3
  18.6 0.0 collective-permute-done.4.refs_1_.refs_6_
  18.6 0.1 collective-permute-start.5
  18.7 0.0 copy-done.2
  18.7 0.1 constant_dynamic-slice_fusion.3
  18.8 4.8 %collective-permute-done.5.refs_7_ = bf16[128,512]{1,0:T(8,128)(2,1)S(1)} collective-permute-done((bf16[128,512]{1,0:T(8,128)(2,1)S(1)}, bf16[128,512]{1,0:T(8,128)(2,1)S(1)}, u32[]{:S(2)}, u32[]{:S(2)}) %collective-permute-start.5) | collective-permute-done | bytes 131104 | tf_op jit(solution)/shard_map/ppermute | solution.py:29
  23.7 0.0 collective-permute-start.8
  23.7 0.0 collective-permute-done.refs_1_
  23.7 0.0 collective-permute-done.1.refs_2_
  23.7 0.0 collective-permute-done.2.refs_3_
  23.8 0.0 collective-permute-done.6.refs_8_
  23.8 0.6 %collective-permute-start.9 = (bf16[32,512]{1,0:T(8,128)(2,1)S(1)}, bf16[32,512]{1,0:T(8,128)(2,1)S(1)}, u32[]{:S(2)}, u32[]{:S(2)}) collective-permute-start(bf16[32,512]{1,0:T(8,128)(2,1)S(1)} %collective-permute-done.6.refs_8_), channel_id=1, source_target_pairs={{0,4},{4,0},{1,5},{5,1},{2,6},{6,2},{3,7},{7,3},{8,12},{12,8},{9,1... | collective-permute-start | bytes 98312 | tf_op jit(solution)/shard_map/ppermute | solution.py:19
  24.3 0.1 collective-permute-start.7
  24.5 0.7 %collective-permute-done.9.refs_11_ = bf16[32,512]{1,0:T(8,128)(2,1)S(1)} collective-permute-done((bf16[32,512]{1,0:T(8,128)(2,1)S(1)}, bf16[32,512]{1,0:T(8,128)(2,1)S(1)}, u32[]{:S(2)}, u32[]{:S(2)}) %collective-permute-start.9) | collective-permute-done | bytes 32800 | tf_op jit(solution)/shard_map/ppermute | solution.py:19
  25.2 0.4 collective-permute-done.7.refs_9_
  25.6 0.0 collective-permute-done.8.refs_10_
  25.6 0.9 %select.5 = (bf16[32,1536]{1,0:T(8,128)(2,1)S(1)}, bf16[32,1536]{1,0:T(8,128)(2,1)S(1)}, bf16[32,1536]{1,0:T(8,128)(2,1)S(1)}, bf16[32,1536]{1,0:T(8,128)(2,1)S(1)}) custom-call(s32[4,128]{1,0:T(4,128)S(1)} %select_select_fusion.listed, s32[8,256]{1,0:T(8,128)S(1)} %get-tuple-element.31.refs_0_, s32[8,256]{1,0:T(8,128)S(1)} %collective-permute-done.refs_1_, ...), custom_call_target="tpu_custom_call" | custom-call | tf_op jit(solution)/shard_map/select/pallas_call | solution.py:195
  26.6 0.5 %collective-permute-start.10 = (bf16[32,1536]{1,0:T(8,128)(2,1)S(1)}, bf16[32,1536]{1,0:T(8,128)(2,1)S(1)}, u32[]{:S(2)}, u32[]{:S(2)}) collective-permute-start(bf16[32,1536]{1,0:T(8,128)(2,1)S(1)} %get-tuple-element.36), channel_id=1, source_target_pairs={{0,64},{64,0},{128,192},{192,128},{1,65},{65,1},{129,193},{193,129... | collective-permute-start | bytes 294920 | tf_op jit(solution)/shard_map/ppermute | solution.py:23
  27.1 3.8 %collective-permute-start.11 = (bf16[32,1536]{1,0:T(8,128)(2,1)S(1)}, bf16[32,1536]{1,0:T(8,128)(2,1)S(1)}, u32[]{:S(2)}, u32[]{:S(2)}) collective-permute-start(bf16[32,1536]{1,0:T(8,128)(2,1)S(1)} %get-tuple-element.37), channel_id=1, source_target_pairs={{0,128},{64,192},{128,0},{192,64},{1,129},{65,193},{129,1},{193,65... | collective-permute-start | bytes 294920 | tf_op jit(solution)/shard_map/ppermute | solution.py:23
  30.9 0.4 collective-permute-start.12
  31.4 0.6 %collective-permute-done.10.one = bf16[32,1536]{1,0:T(8,128)(2,1)S(1)} collective-permute-done((bf16[32,1536]{1,0:T(8,128)(2,1)S(1)}, bf16[32,1536]{1,0:T(8,128)(2,1)S(1)}, u32[]{:S(2)}, u32[]{:S(2)}) %collective-permute-start.10) | collective-permute-done | bytes 98336 | tf_op jit(solution)/shard_map/ppermute | solution.py:23
  32.0 4.2 %collective-permute-done.11.two = bf16[32,1536]{1,0:T(8,128)(2,1)S(1)} collective-permute-done((bf16[32,1536]{1,0:T(8,128)(2,1)S(1)}, bf16[32,1536]{1,0:T(8,128)(2,1)S(1)}, u32[]{:S(2)}, u32[]{:S(2)}) %collective-permute-start.11) | collective-permute-done | bytes 98336 | tf_op jit(solution)/shard_map/ppermute | solution.py:23
  36.2 2.0 %collective-permute-done.12.three = bf16[32,1536]{1,0:T(8,128)(2,1)S(1)} collective-permute-done((bf16[32,1536]{1,0:T(8,128)(2,1)S(1)}, bf16[32,1536]{1,0:T(8,128)(2,1)S(1)}, u32[]{:S(2)}, u32[]{:S(2)}) %collective-permute-start.12) | collective-permute-done | bytes 98336 | tf_op jit(solution)/shard_map/ppermute | solution.py:23
  38.2 0.4 aggregate.1
  38.6 1.7 %collective-permute-start.13 = (bf16[32,640]{1,0:T(8,128)(2,1)S(1)}, bf16[32,640]{1,0:T(8,128)(2,1)S(1)}, u32[]{:S(2)}, u32[]{:S(2)}) collective-permute-start(bf16[32,640]{1,0:T(8,128)(2,1)S(1)} %get-tuple-element.43), channel_id=1, source_target_pairs={{0,1},{1,0},{2,3},{3,2},{4,5},{5,4},{6,7},{7,6},{8,9},{9,8},{10,11... | collective-permute-start | bytes 122888 | tf_op jit(solution)/shard_map/ppermute | solution.py:23
  40.3 2.9 %collective-permute-start.14 = (bf16[32,640]{1,0:T(8,128)(2,1)S(1)}, bf16[32,640]{1,0:T(8,128)(2,1)S(1)}, u32[]{:S(2)}, u32[]{:S(2)}) collective-permute-start(bf16[32,640]{1,0:T(8,128)(2,1)S(1)} %get-tuple-element.44), channel_id=1, source_target_pairs={{0,2},{1,3},{2,0},{3,1},{4,6},{5,7},{6,4},{7,5},{8,10},{9,11},{10,... | collective-permute-start | bytes 122888 | tf_op jit(solution)/shard_map/ppermute | solution.py:23
  43.2 0.2 collective-permute-start.15
  43.4 0.0 copy-done.3
  43.4 0.1 copy.9.refs_4_
  43.5 0.0 collective-permute-done.13.refs_1_
  43.5 2.3 %collective-permute-done.14.refs_2_ = bf16[32,640]{1,0:T(8,128)(2,1)S(1)} collective-permute-done((bf16[32,640]{1,0:T(8,128)(2,1)S(1)}, bf16[32,640]{1,0:T(8,128)(2,1)S(1)}, u32[]{:S(2)}, u32[]{:S(2)}) %collective-permute-start.14) | collective-permute-done | bytes 40992 | tf_op jit(solution)/shard_map/ppermute | solution.py:23
  45.8 2.6 %collective-permute-done.15.refs_3_ = bf16[32,640]{1,0:T(8,128)(2,1)S(1)} collective-permute-done((bf16[32,640]{1,0:T(8,128)(2,1)S(1)}, bf16[32,640]{1,0:T(8,128)(2,1)S(1)}, u32[]{:S(2)}, u32[]{:S(2)}) %collective-permute-start.15) | collective-permute-done | bytes 40992 | tf_op jit(solution)/shard_map/ppermute | solution.py:23
  48.4 0.9 %mix.1 = bf16[64,512]{1,0:T(8,128)(2,1)} custom-call(bf16[32,640]{1,0:T(8,128)(2,1)S(1)} %get-tuple-element.42.refs_0_, bf16[32,640]{1,0:T(8,128)(2,1)S(1)} %collective-permute-done.13.refs_1_, bf16[32,640]{1,0:T(8,128)(2,1)S(1)} %collective-permute-done.14.refs_2_, bf16[32,640]{1,0:T(8,128)(2,1)S(1)} %collective-permute-done.15.refs_3_, ...), custom_call_target="tpu_custom_call" | custom-call | tf_op jit(solution)/shard_map/mix/pallas_call | solution.py:278
  (10 shorter events, 0.1 us)
Async XLA Ops:
  2.7 0.8 %copy-start = (bf16[512,512]{1,0:T(8,128)(2,1)}, bf16[512,512]{1,0:T(8,128)(2,1)S(1)}, u32[]{:S(2)}) copy-start(bf16[512,512]{1,0:T(8,128)(2,1)S(1)} %get-tuple-element.28.self_mask) | copy-start | bytes 1572868
  3.5 15.2 %copy-start.2 = (bf16[32,256]{1,0:T(8,128)(2,1)S(1)}, bf16[32,256]{1,0:T(8,128)(2,1)}, u32[]{:S(2)}) copy-start(bf16[32,256]{1,0:T(8,128)(2,1)} %param.9) | copy-start | bytes 49156
  3.5 1.2 %collective-permute-start.3 = (bf16[32,512]{1,0:T(8,128)(2,1)S(1)}, bf16[32,512]{1,0:T(8,128)(2,1)S(1)}, u32[]{:S(2)}, u32[]{:S(2)}) collective-permute-start(bf16[32,512]{1,0:T(8,128)(2,1)S(1)} %get-tuple-element.29.scaled.refs_0_.refs_4_), channel_id=1, source_target_pairs={{0,4},{4,0},{1,5},{5,1},{2,6},{6,2},{3,7},{7,3},{8,12},{12,8},{9,1... | collective-permute-start | bytes 98312 | tf_op jit(solution)/shard_map/ppermute | solution.py:19
  4.7 13.9 %collective-permute-start.4 = (bf16[64,512]{1,0:T(8,128)(2,1)S(1)}, bf16[64,512]{1,0:T(8,128)(2,1)S(1)}, u32[]{:S(2)}, u32[]{:S(2)}) collective-permute-start(bf16[64,512]{1,0:T(8,128)(2,1)S(1)} %join.2.refs_0_), channel_id=1, source_target_pairs={{0,16},{4,52},{8,24},{12,60},{16,32},{20,4},{24,40},{28,12},{32,48... | collective-permute-start | bytes 196616 | tf_op jit(solution)/shard_map/ppermute | solution.py:29
  8.0 15.7 %collective-permute-start = (s32[8,256]{1,0:T(8,128)S(1)}, s32[8,256]{1,0:T(8,128)S(1)}, u32[]{:S(2)}, u32[]{:S(2)}) collective-permute-start(s32[8,256]{1,0:T(8,128)S(1)} %get-tuple-element.31.refs_0_), channel_id=1, source_target_pairs={{0,64},{64,0},{128,192},{192,128},{1,65},{65,1},{129,193},{193,129... | collective-permute-start | bytes 24584 | tf_op jit(solution)/shard_map/ppermute | solution.py:23
  9.3 14.3 %collective-permute-start.1 = (s32[8,256]{1,0:T(8,128)S(1)}, s32[8,256]{1,0:T(8,128)S(1)}, u32[]{:S(2)}, u32[]{:S(2)}) collective-permute-start(s32[8,256]{1,0:T(8,128)S(1)} %get-tuple-element.31.refs_0_), channel_id=1, source_target_pairs={{0,128},{64,192},{128,0},{192,64},{1,129},{65,193},{129,1},{193,65... | collective-permute-start | bytes 24584 | tf_op jit(solution)/shard_map/ppermute | solution.py:23
  11.6 12.1 %collective-permute-start.2 = (s32[8,256]{1,0:T(8,128)S(1)}, s32[8,256]{1,0:T(8,128)S(1)}, u32[]{:S(2)}, u32[]{:S(2)}) collective-permute-start(s32[8,256]{1,0:T(8,128)S(1)} %get-tuple-element.31.refs_0_), channel_id=1, source_target_pairs={{0,192},{64,128},{128,64},{192,0},{1,193},{65,129},{129,65},{193,1... | collective-permute-start | bytes 24584 | tf_op jit(solution)/shard_map/ppermute | solution.py:23
  12.7 11.1 %collective-permute-start.6 = (bf16[32,512]{1,0:T(8,128)(2,1)S(1)}, bf16[32,512]{1,0:T(8,128)(2,1)S(1)}, u32[]{:S(2)}, u32[]{:S(2)}) collective-permute-start(bf16[32,512]{1,0:T(8,128)(2,1)S(1)} %get-tuple-element.29.scaled.refs_0_.refs_4_), channel_id=1, source_target_pairs={{0,32},{8,40},{16,48},{24,56},{32,0},{40,8},{48,16},{56,24},{1,33}... | collective-permute-start | bytes 98312 | tf_op jit(solution)/shard_map/ppermute | solution.py:19
  17.1 1.0 %copy-start.1 = (bf16[512,512]{1,0:T(8,128)(2,1)S(1)}, bf16[512,512]{1,0:T(8,128)(2,1)}, u32[]{:S(2)}) copy-start(bf16[512,512]{1,0:T(8,128)(2,1)} %copy-done) | copy-start | bytes 1572868
  18.6 24.8 %copy-start.3 = (f32[64]{0:T(128)S(1)}, f32[64]{0:T(128)}, u32[]{:S(2)}) copy-start(f32[64]{0:T(128)} %param.10) | copy-start | bytes 772
  18.6 5.0 %collective-permute-start.5 = (bf16[128,512]{1,0:T(8,128)(2,1)S(1)}, bf16[128,512]{1,0:T(8,128)(2,1)S(1)}, u32[]{:S(2)}, u32[]{:S(2)}) collective-permute-start(bf16[128,512]{1,0:T(8,128)(2,1)S(1)} %join.3), channel_id=1, source_target_pairs={{0,8},{4,60},{8,16},{12,4},{16,24},{20,12},{24,32},{28,20},{32,40}... | collective-permute-start | bytes 393224 | tf_op jit(solution)/shard_map/ppermute | solution.py:29
  23.7 1.9 %collective-permute-start.8 = (bf16[128,512]{1,0:T(8,128)(2,1)S(1)}, bf16[128,512]{1,0:T(8,128)(2,1)S(1)}, u32[]{:S(2)}, u32[]{:S(2)}) collective-permute-start(bf16[128,512]{1,0:T(8,128)(2,1)S(1)} %collective-permute-done.5.refs_7_), channel_id=1, source_target_pairs={{0,4},{4,0},{1,5},{5,1},{2,6},{6,2},{3,7},{7,3},{8,12},{12,8},{9,1... | collective-permute-start | bytes 393224 | tf_op jit(solution)/shard_map/ppermute | solution.py:19
  23.8 1.4 %collective-permute-start.9 = (bf16[32,512]{1,0:T(8,128)(2,1)S(1)}, bf16[32,512]{1,0:T(8,128)(2,1)S(1)}, u32[]{:S(2)}, u32[]{:S(2)}) collective-permute-start(bf16[32,512]{1,0:T(8,128)(2,1)S(1)} %collective-permute-done.6.refs_8_), channel_id=1, source_target_pairs={{0,4},{4,0},{1,5},{5,1},{2,6},{6,2},{3,7},{7,3},{8,12},{12,8},{9,1... | collective-permute-start | bytes 98312 | tf_op jit(solution)/shard_map/ppermute | solution.py:19
  24.3 1.3 %collective-permute-start.7 = (bf16[64,512]{1,0:T(8,128)(2,1)S(1)}, bf16[64,512]{1,0:T(8,128)(2,1)S(1)}, u32[]{:S(2)}, u32[]{:S(2)}) collective-permute-start(bf16[64,512]{1,0:T(8,128)(2,1)S(1)} %collective-permute-done.4.refs_1_.refs_6_), channel_id=1, source_target_pairs={{0,4},{4,0},{1,5},{5,1},{2,6},{6,2},{3,7},{7,3},{8,12},{12,8},{9,1... | collective-permute-start | bytes 196616 | tf_op jit(solution)/shard_map/ppermute | solution.py:19
  26.6 5.4 %collective-permute-start.10 = (bf16[32,1536]{1,0:T(8,128)(2,1)S(1)}, bf16[32,1536]{1,0:T(8,128)(2,1)S(1)}, u32[]{:S(2)}, u32[]{:S(2)}) collective-permute-start(bf16[32,1536]{1,0:T(8,128)(2,1)S(1)} %get-tuple-element.36), channel_id=1, source_target_pairs={{0,64},{64,0},{128,192},{192,128},{1,65},{65,1},{129,193},{193,129... | collective-permute-start | bytes 294920 | tf_op jit(solution)/shard_map/ppermute | solution.py:23
  27.1 9.1 %collective-permute-start.11 = (bf16[32,1536]{1,0:T(8,128)(2,1)S(1)}, bf16[32,1536]{1,0:T(8,128)(2,1)S(1)}, u32[]{:S(2)}, u32[]{:S(2)}) collective-permute-start(bf16[32,1536]{1,0:T(8,128)(2,1)S(1)} %get-tuple-element.37), channel_id=1, source_target_pairs={{0,128},{64,192},{128,0},{192,64},{1,129},{65,193},{129,1},{193,65... | collective-permute-start | bytes 294920 | tf_op jit(solution)/shard_map/ppermute | solution.py:23
  30.9 7.3 %collective-permute-start.12 = (bf16[32,1536]{1,0:T(8,128)(2,1)S(1)}, bf16[32,1536]{1,0:T(8,128)(2,1)S(1)}, u32[]{:S(2)}, u32[]{:S(2)}) collective-permute-start(bf16[32,1536]{1,0:T(8,128)(2,1)S(1)} %get-tuple-element.38), channel_id=1, source_target_pairs={{0,192},{64,128},{128,64},{192,0},{1,193},{65,129},{129,65},{193,1... | collective-permute-start | bytes 294920 | tf_op jit(solution)/shard_map/ppermute | solution.py:23
  38.6 4.9 %collective-permute-start.13 = (bf16[32,640]{1,0:T(8,128)(2,1)S(1)}, bf16[32,640]{1,0:T(8,128)(2,1)S(1)}, u32[]{:S(2)}, u32[]{:S(2)}) collective-permute-start(bf16[32,640]{1,0:T(8,128)(2,1)S(1)} %get-tuple-element.43), channel_id=1, source_target_pairs={{0,1},{1,0},{2,3},{3,2},{4,5},{5,4},{6,7},{7,6},{8,9},{9,8},{10,11... | collective-permute-start | bytes 122888 | tf_op jit(solution)/shard_map/ppermute | solution.py:23
  40.3 5.5 %collective-permute-start.14 = (bf16[32,640]{1,0:T(8,128)(2,1)S(1)}, bf16[32,640]{1,0:T(8,128)(2,1)S(1)}, u32[]{:S(2)}, u32[]{:S(2)}) collective-permute-start(bf16[32,640]{1,0:T(8,128)(2,1)S(1)} %get-tuple-element.44), channel_id=1, source_target_pairs={{0,2},{1,3},{2,0},{3,1},{4,6},{5,7},{6,4},{7,5},{8,10},{9,11},{10,... | collective-permute-start | bytes 122888 | tf_op jit(solution)/shard_map/ppermute | solution.py:23
  43.2 5.2 %collective-permute-start.15 = (bf16[32,640]{1,0:T(8,128)(2,1)S(1)}, bf16[32,640]{1,0:T(8,128)(2,1)S(1)}, u32[]{:S(2)}, u32[]{:S(2)}) collective-permute-start(bf16[32,640]{1,0:T(8,128)(2,1)S(1)} %get-tuple-element.45), channel_id=1, source_target_pairs={{0,3},{1,2},{2,1},{3,0},{4,7},{5,6},{6,5},{7,4},{8,11},{9,10},{10,... | collective-permute-start | bytes 122888 | tf_op jit(solution)/shard_map/ppermute | solution.py:23

commit v2 on v1

--- a/solution.py
+++ b/solution.py
@@ -1,3 +1,5 @@
+import functools
+
 import jax
 import jax.numpy as jnp
 from jax import lax
@@ -158,26 +160,44 @@
     )
 
 
-def select_kernel(listed, *refs):
-    requests, pieces, outs, (held, table, arrived) = refs[:4], refs[4:-7], refs[-7:-3], refs[-3:]
-    tables = pltpu.make_async_copy(listed, table, arrived)
-    tables.start()
+def place_kernel(listed, table, arrived):
+    copy = pltpu.make_async_copy(listed, table, arrived)
+    copy.start()
+    copy.wait()
+
+
+def placed(listed):
+    return pl.pallas_call(
+        place_kernel,
+        out_shape=pltpu.SMEM((4, LANES), jnp.int32),
+        in_specs=whole(),
+        out_specs=pl.BlockSpec(memory_space=pltpu.SMEM),
+        scratch_shapes=[pltpu.SemaphoreType.DMA],
+        compiler_params=pltpu.CompilerParams(vmem_limit_bytes=2**20),
+        name="place",
+    )(listed)
+
+
+def select_kernel(dests, table, *refs):
+    if dests == (0,):
+        requests, refs = ((refs[0], 0),), refs[1:]
+    else:
+        requests, refs = ((refs[0], 0), (refs[1], 0), (refs[1], 8)), refs[2:]
+    pieces, outs, held = refs[: -1 - len(dests)], refs[-1 - len(dests) : -1], refs[-1]
     at = 0
     for piece in pieces:
         for k in range(piece.shape[0] // FEATS):
             held[at] = piece[k * FEATS : (k + 1) * FEATS, :].astype(jnp.float32)
             at += 1
-    for out in outs:
+    for dest, (request, top), out in zip(dests, requests, outs):
         out[...] = jnp.zeros_like(out)
-    tables.wait()
-    for k in range(4):
         for s in range(6):
-            which = table[k, s]
+            which = table[dest, s]
 
             @pl.when(which >= 0)
             def _():
                 for g in range(2):
-                    rows = requests[k][s : s + 1, g * LANES : (g + 1) * LANES]
+                    rows = request[top + s : top + s + 1, g * LANES : (g + 1) * LANES]
                     rows = jnp.broadcast_to(rows, (FEATS, LANES))
                     lane = rows & (LANES - 1)
                     block = rows >> 7
@@ -187,24 +207,19 @@
                         took = jnp.take_along_axis(part, lane, axis=1, mode="promise_in_bounds")
                         picked = jnp.where(block == t, took, picked)
                     to = s * 256 + g * LANES
-                    outs[k][:, to : to + LANES] = picked.astype(jnp.bfloat16)
-
-
-def selected(table, requests, pieces):
-    operands = (table, *requests, *pieces)
-    return pl.pallas_call(
-        select_kernel,
-        out_shape=[VMEM((FEATS, 1536), jnp.bfloat16)] * 4,
-        in_specs=whole(len(operands)),
-        out_specs=whole(4),
-        scratch_shapes=[
-            VMEM((16, FEATS, 512), jnp.float32),
-            pltpu.SMEM((4, LANES), jnp.int32),
-            pltpu.SemaphoreType.DMA,
-        ],
-        compiler_params=pltpu.CompilerParams(vmem_limit_bytes=8 * 2**20),
-        name="select",
-    )(*operands)
+                    out[:, to : to + LANES] = picked.astype(jnp.bfloat16)
+
+
+def selected(dests, table, requests, pieces):
+    operands = (*requests, *pieces)
+    return pl.pallas_call(
+        functools.partial(select_kernel, dests),
+        out_shape=[VMEM((FEATS, 1536), jnp.bfloat16)] * len(dests),
+        in_specs=[pl.BlockSpec(memory_space=pltpu.SMEM)] + whole(len(operands)),
+        out_specs=whole(len(dests)),
+        scratch_shapes=[VMEM((16, FEATS, 512), jnp.float32)],
+        compiler_params=pltpu.CompilerParams(vmem_limit_bytes=8 * 2**20),
+    )(pltpu.with_memory_space_constraint(table, pltpu.SMEM), *operands)
 
 
 def join_kernel(*refs):
@@ -264,30 +279,47 @@
     )(*vals, turned, begun, root, columns)
 
 
-def mix_kernel(*refs):
-    parts, bias, out = refs[:4], refs[4], refs[5]
-    mixed = jnp.broadcast_to(bias[...], (64, 512))
-    for part in parts:
-        mixed = mixed + lax.dot_general(
-            part[:, 512 : 512 + 64], part[:, :512], (((0,), (0,)), ((), ())), preferred_element_type=jnp.float32
-        )
-    out[...] = jnp.maximum(mixed, 0.0).astype(jnp.bfloat16)
-
-
-def mix(parts, bias):
+def mixed(part):
+    return lax.dot_general(
+        part[:, 512:576], part[:, :512], (((0,), (0,)), ((), ())), preferred_element_type=jnp.float32
+    )
+
+
+def mix_kernel(bias, one, two, three, out):
+    out[...] = bias[...] + mixed(one) + mixed(two) + mixed(three)
+
+
+def finish_kernel(begun, part, out):
+    out[...] = jnp.maximum(begun[...] + mixed(part), 0.0).astype(jnp.bfloat16)
+
+
+def mix(bias, parts):
     return pl.pallas_call(
         mix_kernel,
+        out_shape=VMEM((64, 512), jnp.float32),
+        in_specs=whole(4),
+        out_specs=whole()[0],
+        compiler_params=pltpu.CompilerParams(vmem_limit_bytes=8 * 2**20),
+        name="mix",
+    )(bias.reshape(64, 1), *parts)
+
+
+def finish(begun, part):
+    return pl.pallas_call(
+        finish_kernel,
         out_shape=jax.ShapeDtypeStruct((64, 512), jnp.bfloat16),
-        in_specs=whole(5),
-        out_specs=whole(1)[0],
-        compiler_params=pltpu.CompilerParams(vmem_limit_bytes=8 * 2**20),
-        name="mix",
-    )(*parts, bias.reshape(64, 1))
-
-
-def piece_table(requests):
+        in_specs=whole(2),
+        out_specs=whole()[0],
+        compiler_params=pltpu.CompilerParams(vmem_limit_bytes=8 * 2**20),
+        name="finish",
+    )(begun, part)
+
+
+def piece_table(request, beside, across):
     my_x, my_z, my_core = (lax.axis_index(a) for a in VERT)
-    wanted = jnp.concatenate([r[6:7, :LANES] for r in requests], axis=0)
+    wanted = jnp.concatenate(
+        [r[top + 6 : top + 7, :LANES] for r, top in ((request, 0), (beside, 0), (across, 0), (across, 8))], axis=0
+    )
     ahead = (wanted >> 1) - my_z
     ahead = jnp.where(my_core == 0, -ahead, ahead) & 7
     same = (wanted & 1) == my_core
@@ -306,23 +338,26 @@
     partner = shifted(scaled, "core", 1)
     both = joined(scaled, partner)
     two = opposed(both, 2)
-    turned, begun = prepared(held_halo, held_self, scaled)
-    weight, bias, _ = lax.optimization_barrier((weight, bias, begun))
     four = shifted(scaled, "z", 4)
     one = opposed(joined(both, two), 1)
-    requests = [request]
-    for k in (1, 2, 3):
-        requests.append(paired(request, "x", k))
-    *requests, _ = lax.optimization_barrier((*requests, begun))
-    table = piece_table(requests)
+    beside = paired(request, "x", 1)
+    late_request, late_beside, _ = lax.optimization_barrier((request, beside, two))
+    across = paired(jnp.concatenate([late_request, late_beside], axis=0), "x", 3)
+    table = piece_table(request, beside, across)
     rest = []
     for piece in (two, one, four):
         rest.append(shifted(piece, "core", 1))
-    picked = selected(table, requests, (scaled, partner, two, one, four, *rest))
-    vals = [picked[0]]
-    for k in (1, 2, 3):
-        vals.append(paired(picked[k], "x", k))
-
+    table = placed(table)
+    pieces = (scaled, partner, two, one, four, *rest)
+    picked = selected((1, 2, 3), table, (beside, across), pieces)
+    vals = []
+    for at, k in enumerate((1, 3, 2)):
+        vals.append(paired(picked[at], "x", k))
+    vals += selected((0,), table, (request,), pieces)
+
+    held_halo, held_self, _ = lax.optimization_barrier((held_halo, held_self, picked[0]))
+    turned, begun = prepared(held_halo, held_self, scaled)
+    weight, bias, _ = lax.optimization_barrier((weight, bias, picked[0]))
     my_af = lax.axis_index("af")
     columns = jnp.stack(
         [
@@ -332,9 +367,10 @@
     )
     sent = aggregate(vals, turned, begun, root, columns)
     parts = [sent[0]]
-    for k in (1, 2, 3):
+    for k in (2, 3, 1):
         parts.append(paired(sent[k], "af", k))
-    return mix(parts, bias)
+    begun = mix(bias, parts[:3])
+    return finish(begun, parts[3])
 
 
 def solution(mesh):

time: 50.2 us -> 45.1 us (0.90)
  the two profiles are of different devices: /device:TPU:32 before, /device:TPU:2 now
where the time goes in v2:
time: 45.1 us; the launch traced here: 45 us
  starting transfers between devices  21 us (47%)
  waiting for transfers between devices  17.9 us (40%)
  Pallas kernels  5.64 us (13%)
    ppermute x8, starting transfers between devices, paired(): lax.ppermute(array, axis, [(i, i ^ by) for i in range(lax.axis_size(axis))])  11.9 us
    ppermute x8, waiting for transfers between devices, paired(): lax.ppermute(array, axis, [(i, i ^ by) for i in range(lax.axis_size(axis))])  9.42 us
    ppermute x5, starting transfers between devices, shifted(): lax.ppermute(array, axis, [(i, (i + by) % count) for i in range(count)])  5.73 us
    ppermute x2, waiting for transfers between devices, opposed(): return lax.ppermute(array, ('z', 'core'), pairs)  5.27 us
    ppermute x2, starting transfers between devices, opposed(): return lax.ppermute(array, ('z', 'core'), pairs)  3.4 us
    ppermute x5, waiting for transfers between devices, shifted(): lax.ppermute(array, axis, [(i, (i + by) % count) for i in range(count)])  3.24 us
    pallas_call x1, Pallas kernels, head(): pl.pallas_call(head_kernel, out_shape=[VMEM((FEATS, 512), jnp.bfloat16),...  2.56 us
  transfers between devices with their start and end apart: 15, of which 9 were waited for; matrix products, arithmetic and copies ran while one was open for 1% of the time, Pallas kernels for 3%

profile of v2, /device:TPU:2, one launch (start us, length us, event | category | flops | bytes accessed | tf_op | source)
XLA Modules:
  0.0 45.0 jit_solution(8073292155304633541)
XLA Ops:
  0.0 2.6 %head.1 = (bf16[32,512]{1,0:T(8,128)(2,1)S(1)}, f32[1,512]{1,0:T(1,128)S(1)}, s32[8,256]{1,0:T(8,128)S(1)}, bf16[512,512]{1,0:T(8,128)(2,1)S(1)}, bf16[6,512,256]{2,1,0:T(8,128)(2,1)S(1)}) custom-call(s32[1,6]{1,0:T(1,128)} %sources_in.1, s32[1,512,512]{2,1,0:T(8,128)} %self_in.1, s32[1,6,512,256]{3,2,1,0:T(8,128)} %halo_in.1, s32[1,512]{1,0:T(1,128)} %bitcast.12, ...), custom_call_target="tpu_custom_call" | custom-call | tf_op jit(solution)/shard_map/head/pallas_call | solution.py:123
  2.6 0.0 copy-start
  2.6 0.1 collective-permute-start.1
  2.7 1.2 %collective-permute-done.1.refs_1_.refs_3_.refs_2_ = bf16[32,512]{1,0:T(8,128)(2,1)S(1)} collective-permute-done((bf16[32,512]{1,0:T(8,128)(2,1)S(1)}, bf16[32,512]{1,0:T(8,128)(2,1)S(1)}, u32[]{:S(2)}, u32[]{:S(2)}) %collective-permute-start.1) | collective-permute-done | bytes 32800 | tf_op jit(solution)/shard_map/ppermute | solution.py:21
  3.9 2.9 %collective-permute-start.2 = (bf16[64,512]{1,0:T(8,128)(2,1)S(1)}, bf16[64,512]{1,0:T(8,128)(2,1)S(1)}, u32[]{:S(2)}, u32[]{:S(2)}) collective-permute-start(bf16[64,512]{1,0:T(8,128)(2,1)S(1)} %join.2.refs_0_), channel_id=1, source_target_pairs={{0,16},{4,52},{8,24},{12,60},{16,32},{20,4},{24,40},{28,12},{32,48... | collective-permute-start | bytes 196616 | tf_op jit(solution)/shard_map/ppermute | solution.py:31
  6.8 0.5 %collective-permute-start = (s32[8,256]{1,0:T(8,128)S(1)}, s32[8,256]{1,0:T(8,128)S(1)}, u32[]{:S(2)}, u32[]{:S(2)}) collective-permute-start(s32[8,256]{1,0:T(8,128)S(1)} %get-tuple-element.27.refs_0_), channel_id=1, source_target_pairs={{0,64},{64,0},{128,192},{192,128},{1,65},{65,1},{129,193},{193,129... | collective-permute-start | bytes 24584 | tf_op jit(solution)/shard_map/ppermute | solution.py:25
  7.3 5.3 %collective-permute-done.2.refs_1_.refs_4_.refs_3_ = bf16[64,512]{1,0:T(8,128)(2,1)S(1)} collective-permute-done((bf16[64,512]{1,0:T(8,128)(2,1)S(1)}, bf16[64,512]{1,0:T(8,128)(2,1)S(1)}, u32[]{:S(2)}, u32[]{:S(2)}) %collective-permute-start.2) | collective-permute-done | bytes 65568 | tf_op jit(solution)/shard_map/ppermute | solution.py:31
  12.6 0.5 %collective-permute-start.4 = (bf16[128,512]{1,0:T(8,128)(2,1)S(1)}, bf16[128,512]{1,0:T(8,128)(2,1)S(1)}, u32[]{:S(2)}, u32[]{:S(2)}) collective-permute-start(bf16[128,512]{1,0:T(8,128)(2,1)S(1)} %join.3), channel_id=1, source_target_pairs={{0,8},{4,60},{8,16},{12,4},{16,24},{20,12},{24,32},{28,20},{32,40}... | collective-permute-start | bytes 393224 | tf_op jit(solution)/shard_map/ppermute | solution.py:31
  13.1 5.0 %collective-permute-start.5 = (bf16[32,512]{1,0:T(8,128)(2,1)S(1)}, bf16[32,512]{1,0:T(8,128)(2,1)S(1)}, u32[]{:S(2)}, u32[]{:S(2)}) collective-permute-start(bf16[32,512]{1,0:T(8,128)(2,1)S(1)} %get-tuple-element.26.refs_0_.refs_2_.refs_1_.scaled), channel_id=1, source_target_pairs={{0,32},{8,40},{16,48},{24,56},{32,0},{40,8},{48,16},{56,24},{1,33}... | collective-permute-start | bytes 98312 | tf_op jit(solution)/shard_map/ppermute | solution.py:21
  18.1 0.0 collective-permute-done.refs_0_
  18.1 2.2 %collective-permute-start.3 = (s32[16,256]{1,0:T(8,128)S(1)}, s32[16,256]{1,0:T(8,128)S(1)}, u32[]{:S(2)}, u32[]{:S(2)}) collective-permute-start(s32[16,256]{1,0:T(8,128)S(1)} %pad_add_fusion), channel_id=1, source_target_pairs={{0,192},{64,128},{128,64},{192,0},{1,193},{65,129},{129,65},{193,1... | collective-permute-start | bytes 49160 | tf_op jit(solution)/shard_map/ppermute | solution.py:25
  20.3 1.4 %collective-permute-done.5.refs_6_.refs_5_ = bf16[32,512]{1,0:T(8,128)(2,1)S(1)} collective-permute-done((bf16[32,512]{1,0:T(8,128)(2,1)S(1)}, bf16[32,512]{1,0:T(8,128)(2,1)S(1)}, u32[]{:S(2)}, u32[]{:S(2)}) %collective-permute-start.5) | collective-permute-done | bytes 32800 | tf_op jit(solution)/shard_map/ppermute | solution.py:21
  21.7 0.1 collective-permute-start.8
  21.9 0.4 collective-permute-start.6
  22.3 0.0 collective-permute-done.4.refs_5_.refs_4_
  22.3 0.1 collective-permute-start.7
  22.4 0.0 collective-permute-done.3.refs_1_
  22.4 0.6 %place.1.table = s32[4,128]{1,0:T(4,128)S(4)} custom-call(s32[4,128]{1,0:T(4,128)S(1)} %select_select_fusion.listed), custom_call_target="tpu_custom_call" | custom-call | tf_op jit(solution)/shard_map/place/pallas_call | solution.py:170
  23.0 0.0 collective-permute-done.8.refs_9_.refs_8_
  23.0 0.2 collective-permute-done.6.refs_7_.refs_6_
  23.2 0.4 collective-permute-done.7.refs_8_.refs_7_
  23.6 0.5 %shard_map.82 = (bf16[32,1536]{1,0:T(8,128)(2,1)S(1)}, bf16[32,1536]{1,0:T(8,128)(2,1)S(1)}, bf16[32,1536]{1,0:T(8,128)(2,1)S(1)}) custom-call(s32[4,128]{1,0:T(4,128)S(4)} %place.1.table, s32[8,256]{1,0:T(8,128)S(1)} %collective-permute-done.refs_0_, s32[16,256]{1,0:T(8,128)S(1)} %collective-permute-done.3.refs_1_, ...), custom_call_target="tpu_custom_call" | custom-call | tf_op jit(solution)/shard_map/pallas_call | solution.py:215
  24.1 1.5 %collective-permute-start.9 = (bf16[32,1536]{1,0:T(8,128)(2,1)S(1)}, bf16[32,1536]{1,0:T(8,128)(2,1)S(1)}, u32[]{:S(2)}, u32[]{:S(2)}) collective-permute-start(bf16[32,1536]{1,0:T(8,128)(2,1)S(1)} %get-tuple-element.29), channel_id=1, source_target_pairs={{0,64},{64,0},{128,192},{192,128},{1,65},{65,1},{129,193},{193,129... | collective-permute-start | bytes 294920 | tf_op jit(solution)/shard_map/ppermute | solution.py:25
  25.5 3.4 %collective-permute-start.10 = (bf16[32,1536]{1,0:T(8,128)(2,1)S(1)}, bf16[32,1536]{1,0:T(8,128)(2,1)S(1)}, u32[]{:S(2)}, u32[]{:S(2)}) collective-permute-start(bf16[32,1536]{1,0:T(8,128)(2,1)S(1)} %get-tuple-element.31), channel_id=1, source_target_pairs={{0,192},{64,128},{128,64},{192,0},{1,193},{65,129},{129,65},{193,1... | collective-permute-start | bytes 294920 | tf_op jit(solution)/shard_map/ppermute | solution.py:25
  28.9 0.0 collective-permute-start.11
  28.9 0.5 %prepare.1 = (bf16[1536,512]{1,0:T(8,128)(2,1)S(1)}, f32[32,512]{1,0:T(8,128)S(1)}) custom-call(bf16[6,512,256]{2,1,0:T(8,128)(2,1)S(1)} %get-tuple-element.35.halo_mask, bf16[512,512]{1,0:T(8,128)(2,1)S(1)} %get-tuple-element.36.self_mask, bf16[32,512]{1,0:T(8,128)(2,1)S(1)} %get-tuple-element.26.refs_0_.refs_2_.refs_1_.scaled), custom_call_target="tpu_custom_call" | custom-call | tf_op jit(solution)/shard_map/prepare/pallas_call | solution.py:252
  29.4 0.0 copy-done
  29.4 0.0 copy-start.1
  29.4 0.1 constant_dynamic-slice_fusion.3
  29.6 0.1 shard_map.83.three
  29.7 3.5 %collective-permute-done.10.one = bf16[32,1536]{1,0:T(8,128)(2,1)S(1)} collective-permute-done((bf16[32,1536]{1,0:T(8,128)(2,1)S(1)}, bf16[32,1536]{1,0:T(8,128)(2,1)S(1)}, u32[]{:S(2)}, u32[]{:S(2)}) %collective-permute-start.10) | collective-permute-done | bytes 98336 | tf_op jit(solution)/shard_map/ppermute | solution.py:25
  33.2 1.8 %collective-permute-done.11.two = bf16[32,1536]{1,0:T(8,128)(2,1)S(1)} collective-permute-done((bf16[32,1536]{1,0:T(8,128)(2,1)S(1)}, bf16[32,1536]{1,0:T(8,128)(2,1)S(1)}, u32[]{:S(2)}, u32[]{:S(2)}) %collective-permute-start.11) | collective-permute-done | bytes 98336 | tf_op jit(solution)/shard_map/ppermute | solution.py:25
  35.1 0.0 collective-permute-done.9.mine
  35.1 0.4 aggregate.1
  35.5 3.3 %collective-permute-start.12 = (bf16[32,640]{1,0:T(8,128)(2,1)S(1)}, bf16[32,640]{1,0:T(8,128)(2,1)S(1)}, u32[]{:S(2)}, u32[]{:S(2)}) collective-permute-start(bf16[32,640]{1,0:T(8,128)(2,1)S(1)} %get-tuple-element.42), channel_id=1, source_target_pairs={{0,2},{1,3},{2,0},{3,1},{4,6},{5,7},{6,4},{7,5},{8,10},{9,11},{10,... | collective-permute-start | bytes 122888 | tf_op jit(solution)/shard_map/ppermute | solution.py:25
  38.7 1.1 %collective-permute-start.13 = (bf16[32,640]{1,0:T(8,128)(2,1)S(1)}, bf16[32,640]{1,0:T(8,128)(2,1)S(1)}, u32[]{:S(2)}, u32[]{:S(2)}) collective-permute-start(bf16[32,640]{1,0:T(8,128)(2,1)S(1)} %get-tuple-element.43), channel_id=1, source_target_pairs={{0,3},{1,2},{2,1},{3,0},{4,7},{5,6},{6,5},{7,4},{8,11},{9,10},{10,... | collective-permute-start | bytes 122888 | tf_op jit(solution)/shard_map/ppermute | solution.py:25
  39.8 0.0 collective-permute-start.14
  39.8 0.0 copy-done.1
  39.8 0.1 copy.9.bias
  39.9 1.3 %collective-permute-done.12.two = bf16[32,640]{1,0:T(8,128)(2,1)S(1)} collective-permute-done((bf16[32,640]{1,0:T(8,128)(2,1)S(1)}, bf16[32,640]{1,0:T(8,128)(2,1)S(1)}, u32[]{:S(2)}, u32[]{:S(2)}) %collective-permute-start.12) | collective-permute-done | bytes 40992 | tf_op jit(solution)/shard_map/ppermute | solution.py:25
  41.2 2.8 %collective-permute-done.13.three = bf16[32,640]{1,0:T(8,128)(2,1)S(1)} collective-permute-done((bf16[32,640]{1,0:T(8,128)(2,1)S(1)}, bf16[32,640]{1,0:T(8,128)(2,1)S(1)}, u32[]{:S(2)}, u32[]{:S(2)}) %collective-permute-start.13) | collective-permute-done | bytes 40992 | tf_op jit(solution)/shard_map/ppermute | solution.py:25
  44.0 0.2 mix.1.begun
  44.2 0.0 collective-permute-done.14.part
  44.2 0.8 %finish.1 = bf16[64,512]{1,0:T(8,128)(2,1)} custom-call(f32[64,512]{1,0:T(8,128)S(1)} %mix.1.begun, bf16[32,640]{1,0:T(8,128)(2,1)S(1)} %collective-permute-done.14.part), custom_call_target="tpu_custom_call" | custom-call | tf_op jit(solution)/shard_map/finish/pallas_call | solution.py:308
  (10 shorter events, 0.1 us)
Async XLA Ops:
  2.6 26.8 %copy-start = (bf16[32,256]{1,0:T(8,128)(2,1)S(1)}, bf16[32,256]{1,0:T(8,128)(2,1)}, u32[]{:S(2)}) copy-start(bf16[32,256]{1,0:T(8,128)(2,1)} %param.9) | copy-start | bytes 49156
  2.6 1.3 %collective-permute-start.1 = (bf16[32,512]{1,0:T(8,128)(2,1)S(1)}, bf16[32,512]{1,0:T(8,128)(2,1)S(1)}, u32[]{:S(2)}, u32[]{:S(2)}) collective-permute-start(bf16[32,512]{1,0:T(8,128)(2,1)S(1)} %get-tuple-element.26.refs_0_.refs_2_.refs_1_.scaled), channel_id=1, source_target_pairs={{0,4},{4,0},{1,5},{5,1},{2,6},{6,2},{3,7},{7,3},{8,12},{12,8},{9,1... | collective-permute-start | bytes 98312 | tf_op jit(solution)/shard_map/ppermute | solution.py:21
  3.9 8.7 %collective-permute-start.2 = (bf16[64,512]{1,0:T(8,128)(2,1)S(1)}, bf16[64,512]{1,0:T(8,128)(2,1)S(1)}, u32[]{:S(2)}, u32[]{:S(2)}) collective-permute-start(bf16[64,512]{1,0:T(8,128)(2,1)S(1)} %join.2.refs_0_), channel_id=1, source_target_pairs={{0,16},{4,52},{8,24},{12,60},{16,32},{20,4},{24,40},{28,12},{32,48... | collective-permute-start | bytes 196616 | tf_op jit(solution)/shard_map/ppermute | solution.py:31
  6.8 11.3 %collective-permute-start = (s32[8,256]{1,0:T(8,128)S(1)}, s32[8,256]{1,0:T(8,128)S(1)}, u32[]{:S(2)}, u32[]{:S(2)}) collective-permute-start(s32[8,256]{1,0:T(8,128)S(1)} %get-tuple-element.27.refs_0_), channel_id=1, source_target_pairs={{0,64},{64,0},{128,192},{192,128},{1,65},{65,1},{129,193},{193,129... | collective-permute-start | bytes 24584 | tf_op jit(solution)/shard_map/ppermute | solution.py:25
  12.6 9.7 %collective-permute-start.4 = (bf16[128,512]{1,0:T(8,128)(2,1)S(1)}, bf16[128,512]{1,0:T(8,128)(2,1)S(1)}, u32[]{:S(2)}, u32[]{:S(2)}) collective-permute-start(bf16[128,512]{1,0:T(8,128)(2,1)S(1)} %join.3), channel_id=1, source_target_pairs={{0,8},{4,60},{8,16},{12,4},{16,24},{20,12},{24,32},{28,20},{32,40}... | collective-permute-start | bytes 393224 | tf_op jit(solution)/shard_map/ppermute | solution.py:31
  13.1 8.7 %collective-permute-start.5 = (bf16[32,512]{1,0:T(8,128)(2,1)S(1)}, bf16[32,512]{1,0:T(8,128)(2,1)S(1)}, u32[]{:S(2)}, u32[]{:S(2)}) collective-permute-start(bf16[32,512]{1,0:T(8,128)(2,1)S(1)} %get-tuple-element.26.refs_0_.refs_2_.refs_1_.scaled), channel_id=1, source_target_pairs={{0,32},{8,40},{16,48},{24,56},{32,0},{40,8},{48,16},{56,24},{1,33}... | collective-permute-start | bytes 98312 | tf_op jit(solution)/shard_map/ppermute | solution.py:21
  18.1 4.3 %collective-permute-start.3 = (s32[16,256]{1,0:T(8,128)S(1)}, s32[16,256]{1,0:T(8,128)S(1)}, u32[]{:S(2)}, u32[]{:S(2)}) collective-permute-start(s32[16,256]{1,0:T(8,128)S(1)} %pad_add_fusion), channel_id=1, source_target_pairs={{0,192},{64,128},{128,64},{192,0},{1,193},{65,129},{129,65},{193,1... | collective-permute-start | bytes 49160 | tf_op jit(solution)/shard_map/ppermute | solution.py:25
  21.7 1.2 %collective-permute-start.8 = (bf16[32,512]{1,0:T(8,128)(2,1)S(1)}, bf16[32,512]{1,0:T(8,128)(2,1)S(1)}, u32[]{:S(2)}, u32[]{:S(2)}) collective-permute-start(bf16[32,512]{1,0:T(8,128)(2,1)S(1)} %collective-permute-done.5.refs_6_.refs_5_), channel_id=1, source_target_pairs={{0,4},{4,0},{1,5},{5,1},{2,6},{6,2},{3,7},{7,3},{8,12},{12,8},{9,1... | collective-permute-start | bytes 98312 | tf_op jit(solution)/shard_map/ppermute | solution.py:21
  21.9 1.3 %collective-permute-start.6 = (bf16[64,512]{1,0:T(8,128)(2,1)S(1)}, bf16[64,512]{1,0:T(8,128)(2,1)S(1)}, u32[]{:S(2)}, u32[]{:S(2)}) collective-permute-start(bf16[64,512]{1,0:T(8,128)(2,1)S(1)} %collective-permute-done.2.refs_1_.refs_4_.refs_3_), channel_id=1, source_target_pairs={{0,4},{4,0},{1,5},{5,1},{2,6},{6,2},{3,7},{7,3},{8,12},{12,8},{9,1... | collective-permute-start | bytes 196616 | tf_op jit(solution)/shard_map/ppermute | solution.py:21
  22.3 1.3 %collective-permute-start.7 = (bf16[128,512]{1,0:T(8,128)(2,1)S(1)}, bf16[128,512]{1,0:T(8,128)(2,1)S(1)}, u32[]{:S(2)}, u32[]{:S(2)}) collective-permute-start(bf16[128,512]{1,0:T(8,128)(2,1)S(1)} %collective-permute-done.4.refs_5_.refs_4_), channel_id=1, source_target_pairs={{0,4},{4,0},{1,5},{5,1},{2,6},{6,2},{3,7},{7,3},{8,12},{12,8},{9,1... | collective-permute-start | bytes 393224 | tf_op jit(solution)/shard_map/ppermute | solution.py:21
  24.1 11.0 %collective-permute-start.9 = (bf16[32,1536]{1,0:T(8,128)(2,1)S(1)}, bf16[32,1536]{1,0:T(8,128)(2,1)S(1)}, u32[]{:S(2)}, u32[]{:S(2)}) collective-permute-start(bf16[32,1536]{1,0:T(8,128)(2,1)S(1)} %get-tuple-element.29), channel_id=1, source_target_pairs={{0,64},{64,0},{128,192},{192,128},{1,65},{65,1},{129,193},{193,129... | collective-permute-start | bytes 294920 | tf_op jit(solution)/shard_map/ppermute | solution.py:25
  25.5 7.7 %collective-permute-start.10 = (bf16[32,1536]{1,0:T(8,128)(2,1)S(1)}, bf16[32,1536]{1,0:T(8,128)(2,1)S(1)}, u32[]{:S(2)}, u32[]{:S(2)}) collective-permute-start(bf16[32,1536]{1,0:T(8,128)(2,1)S(1)} %get-tuple-element.31), channel_id=1, source_target_pairs={{0,192},{64,128},{128,64},{192,0},{1,193},{65,129},{129,65},{193,1... | collective-permute-start | bytes 294920 | tf_op jit(solution)/shard_map/ppermute | solution.py:25
  28.9 6.1 %collective-permute-start.11 = (bf16[32,1536]{1,0:T(8,128)(2,1)S(1)}, bf16[32,1536]{1,0:T(8,128)(2,1)S(1)}, u32[]{:S(2)}, u32[]{:S(2)}) collective-permute-start(bf16[32,1536]{1,0:T(8,128)(2,1)S(1)} %get-tuple-element.32), channel_id=1, source_target_pairs={{0,128},{64,192},{128,0},{192,64},{1,129},{65,193},{129,1},{193,65... | collective-permute-start | bytes 294920 | tf_op jit(solution)/shard_map/ppermute | solution.py:25
  29.4 10.4 %copy-start.1 = (f32[64]{0:T(128)S(1)}, f32[64]{0:T(128)}, u32[]{:S(2)}) copy-start(f32[64]{0:T(128)} %param.10) | copy-start | bytes 772
  35.5 5.7 %collective-permute-start.12 = (bf16[32,640]{1,0:T(8,128)(2,1)S(1)}, bf16[32,640]{1,0:T(8,128)(2,1)S(1)}, u32[]{:S(2)}, u32[]{:S(2)}) collective-permute-start(bf16[32,640]{1,0:T(8,128)(2,1)S(1)} %get-tuple-element.42), channel_id=1, source_target_pairs={{0,2},{1,3},{2,0},{3,1},{4,6},{5,7},{6,4},{7,5},{8,10},{9,11},{10,... | collective-permute-start | bytes 122888 | tf_op jit(solution)/shard_map/ppermute | solution.py:25
  38.7 5.2 %collective-permute-start.13 = (bf16[32,640]{1,0:T(8,128)(2,1)S(1)}, bf16[32,640]{1,0:T(8,128)(2,1)S(1)}, u32[]{:S(2)}, u32[]{:S(2)}) collective-permute-start(bf16[32,640]{1,0:T(8,128)(2,1)S(1)} %get-tuple-element.43), channel_id=1, source_target_pairs={{0,3},{1,2},{2,1},{3,0},{4,7},{5,6},{6,5},{7,4},{8,11},{9,10},{10,... | collective-permute-start | bytes 122888 | tf_op jit(solution)/shard_map/ppermute | solution.py:25
  39.8 4.4 %collective-permute-start.14 = (bf16[32,640]{1,0:T(8,128)(2,1)S(1)}, bf16[32,640]{1,0:T(8,128)(2,1)S(1)}, u32[]{:S(2)}, u32[]{:S(2)}) collective-permute-start(bf16[32,640]{1,0:T(8,128)(2,1)S(1)} %get-tuple-element.44), channel_id=1, source_target_pairs={{0,1},{1,0},{2,3},{3,2},{4,5},{5,4},{6,7},{7,6},{8,9},{9,8},{10,11... | collective-permute-start | bytes 122888 | tf_op jit(solution)/shard_map/ppermute | solution.py:25

commit v3 on v2

--- a/solution.py
+++ b/solution.py
@@ -72,6 +72,12 @@
     smalls[0].wait()
     for s in range(SURE, 6):
         pl.when(sources[0, s] >= 0)(slots[s].start)
+    for s in range(1, 6):
+
+        def left_out(s=s):
+            halo_out[s] = jnp.zeros_like(halo_out[s])
+
+        pl.when(sources[0, s] < 0)(left_out)
     for copy in smalls[1:]:
         copy.wait()
 
@@ -102,13 +108,8 @@
             halo_out[s] = block.astype(jnp.float32).astype(jnp.bfloat16)
             total[...] += block[:, :LANES] + block[:, LANES:]
 
-        def left_out(s=s):
-            halo_out[s] = jnp.zeros_like(halo_out[s])
-
         if s:
-            live = sources[0, s] >= 0
-            pl.when(live)(counted)
-            pl.when(jnp.logical_not(live))(left_out)
+            pl.when(sources[0, s] >= 0)(counted)
         else:
             counted()
     ones = jnp.ones((8, LANES), jnp.bfloat16)
@@ -357,7 +358,7 @@
 
     held_halo, held_self, _ = lax.optimization_barrier((held_halo, held_self, picked[0]))
     turned, begun = prepared(held_halo, held_self, scaled)
-    weight, bias, _ = lax.optimization_barrier((weight, bias, picked[0]))
+    weight, bias, _ = lax.optimization_barrier((weight, bias, begun))
     my_af = lax.axis_index("af")
     columns = jnp.stack(
         [

time: 45.1 us -> 45.7 us (1.013)
  waiting for transfers between devices: 17.9 us -> 19.2 us
  starting transfers between devices: 21 us -> 20.4 us
    ppermute x5, waiting for transfers between devices: 3.24 us -> 3.93 us  [shifted(): lax.ppermute(array, axis, [(i, (i + by) % count) for i in range(count)])]
    ppermute x8, starting transfers between devices: 11.9 us -> 11.3 us  [paired(): lax.ppermute(array, axis, [(i, i ^ by) for i in range(lax.axis_size(axis))])]
    ppermute x8, waiting for transfers between devices: 9.42 us -> 9.91 us  [paired(): lax.ppermute(array, axis, [(i, i ^ by) for i in range(lax.axis_size(axis))])]
where the time goes in v3:
time: 45.7 us; the launch traced here: 45.6 us
  starting transfers between devices  20.4 us (45%)
  waiting for transfers between devices  19.2 us (42%)
  Pallas kernels  5.62 us (12%)
    ppermute x8, starting transfers between devices, paired(): lax.ppermute(array, axis, [(i, i ^ by) for i in range(lax.axis_size(axis))])  11.3 us
    ppermute x8, waiting for transfers between devices, paired(): lax.ppermute(array, axis, [(i, i ^ by) for i in range(lax.axis_size(axis))])  9.91 us
    ppermute x5, starting transfers between devices, shifted(): lax.ppermute(array, axis, [(i, (i + by) % count) for i in range(count)])  5.73 us
    ppermute x2, waiting for transfers between devices, opposed(): return lax.ppermute(array, ('z', 'core'), pairs)  5.35 us
    ppermute x5, waiting for transfers between devices, shifted(): lax.ppermute(array, axis, [(i, (i + by) % count) for i in range(count)])  3.93 us
    ppermute x2, starting transfers between devices, opposed(): return lax.ppermute(array, ('z', 'core'), pairs)  3.33 us
    pallas_call x1, Pallas kernels, head(): pl.pallas_call(head_kernel, out_shape=[VMEM((FEATS, 512), jnp.bfloat16),...  2.54 us
  transfers between devices with their start and end apart: 15, of which 9 were waited for; matrix products, arithmetic and copies ran while one was open for 1% of the time, Pallas kernels for 3%

profile of v3, /device:TPU:2, one launch (start us, length us, event | category | flops | bytes accessed | tf_op | source)
XLA Modules:
  0.0 45.6 jit_solution(9103999563938775366)
XLA Ops:
  0.0 2.5 %head.1 = (bf16[32,512]{1,0:T(8,128)(2,1)S(1)}, f32[1,512]{1,0:T(1,128)S(1)}, s32[8,256]{1,0:T(8,128)S(1)}, bf16[512,512]{1,0:T(8,128)(2,1)S(1)}, bf16[6,512,256]{2,1,0:T(8,128)(2,1)S(1)}) custom-call(s32[1,6]{1,0:T(1,128)} %sources_in.1, s32[1,512,512]{2,1,0:T(8,128)} %self_in.1, s32[1,6,512,256]{3,2,1,0:T(8,128)} %halo_in.1, s32[1,512]{1,0:T(1,128)} %bitcast.12, ...), custom_call_target="tpu_custom_call" | custom-call | tf_op jit(solution)/shard_map/head/pallas_call | solution.py:124
  2.5 0.0 copy-start
  2.6 0.1 collective-permute-start.1
  2.7 1.2 %collective-permute-done.1.refs_1_.refs_3_.refs_2_ = bf16[32,512]{1,0:T(8,128)(2,1)S(1)} collective-permute-done((bf16[32,512]{1,0:T(8,128)(2,1)S(1)}, bf16[32,512]{1,0:T(8,128)(2,1)S(1)}, u32[]{:S(2)}, u32[]{:S(2)}) %collective-permute-start.1) | collective-permute-done | bytes 32800 | tf_op jit(solution)/shard_map/ppermute | solution.py:21
  3.9 2.9 %collective-permute-start.2 = (bf16[64,512]{1,0:T(8,128)(2,1)S(1)}, bf16[64,512]{1,0:T(8,128)(2,1)S(1)}, u32[]{:S(2)}, u32[]{:S(2)}) collective-permute-start(bf16[64,512]{1,0:T(8,128)(2,1)S(1)} %join.2.refs_0_), channel_id=1, source_target_pairs={{0,16},{4,52},{8,24},{12,60},{16,32},{20,4},{24,40},{28,12},{32,48... | collective-permute-start | bytes 196616 | tf_op jit(solution)/shard_map/ppermute | solution.py:31
  6.8 0.4 collective-permute-start
  7.2 5.3 %collective-permute-done.2.refs_1_.refs_4_.refs_3_ = bf16[64,512]{1,0:T(8,128)(2,1)S(1)} collective-permute-done((bf16[64,512]{1,0:T(8,128)(2,1)S(1)}, bf16[64,512]{1,0:T(8,128)(2,1)S(1)}, u32[]{:S(2)}, u32[]{:S(2)}) %collective-permute-start.2) | collective-permute-done | bytes 65568 | tf_op jit(solution)/shard_map/ppermute | solution.py:31
  12.6 0.4 collective-permute-start.4
  13.0 5.0 %collective-permute-start.5 = (bf16[32,512]{1,0:T(8,128)(2,1)S(1)}, bf16[32,512]{1,0:T(8,128)(2,1)S(1)}, u32[]{:S(2)}, u32[]{:S(2)}) collective-permute-start(bf16[32,512]{1,0:T(8,128)(2,1)S(1)} %get-tuple-element.28.refs_0_.refs_2_.scaled.refs_1_), channel_id=1, source_target_pairs={{0,32},{8,40},{16,48},{24,56},{32,0},{40,8},{48,16},{56,24},{1,33}... | collective-permute-start | bytes 98312 | tf_op jit(solution)/shard_map/ppermute | solution.py:21
  18.0 0.0 collective-permute-done.refs_0_
  18.0 1.5 %collective-permute-start.3 = (s32[16,256]{1,0:T(8,128)S(1)}, s32[16,256]{1,0:T(8,128)S(1)}, u32[]{:S(2)}, u32[]{:S(2)}) collective-permute-start(s32[16,256]{1,0:T(8,128)S(1)} %pad_add_fusion), channel_id=1, source_target_pairs={{0,192},{64,128},{128,64},{192,0},{1,193},{65,129},{129,65},{193,1... | collective-permute-start | bytes 49160 | tf_op jit(solution)/shard_map/ppermute | solution.py:25
  19.5 2.1 %collective-permute-done.5.refs_6_.refs_5_ = bf16[32,512]{1,0:T(8,128)(2,1)S(1)} collective-permute-done((bf16[32,512]{1,0:T(8,128)(2,1)S(1)}, bf16[32,512]{1,0:T(8,128)(2,1)S(1)}, u32[]{:S(2)}, u32[]{:S(2)}) %collective-permute-start.5) | collective-permute-done | bytes 32800 | tf_op jit(solution)/shard_map/ppermute | solution.py:21
  21.7 0.1 collective-permute-start.8
  21.8 0.4 collective-permute-start.6
  22.2 0.0 collective-permute-done.4.refs_5_.refs_4_
  22.2 0.1 collective-permute-start.7
  22.3 0.0 collective-permute-done.3.refs_1_
  22.3 0.6 %place.1.table = s32[4,128]{1,0:T(4,128)S(4)} custom-call(s32[4,128]{1,0:T(4,128)S(1)} %select_select_fusion.listed), custom_call_target="tpu_custom_call" | custom-call | tf_op jit(solution)/shard_map/place/pallas_call | solution.py:171
  22.9 0.0 collective-permute-done.8.refs_9_.refs_8_
  22.9 0.2 collective-permute-done.6.refs_7_.refs_6_
  23.1 0.4 collective-permute-done.7.refs_8_.refs_7_
  23.5 0.5 %shard_map.82 = (bf16[32,1536]{1,0:T(8,128)(2,1)S(1)}, bf16[32,1536]{1,0:T(8,128)(2,1)S(1)}, bf16[32,1536]{1,0:T(8,128)(2,1)S(1)}) custom-call(s32[4,128]{1,0:T(4,128)S(4)} %place.1.table, s32[8,256]{1,0:T(8,128)S(1)} %collective-permute-done.refs_0_, s32[16,256]{1,0:T(8,128)S(1)} %collective-permute-done.3.refs_1_, ...), custom_call_target="tpu_custom_call" | custom-call | tf_op jit(solution)/shard_map/pallas_call | solution.py:216
  24.0 1.5 %collective-permute-start.9 = (bf16[32,1536]{1,0:T(8,128)(2,1)S(1)}, bf16[32,1536]{1,0:T(8,128)(2,1)S(1)}, u32[]{:S(2)}, u32[]{:S(2)}) collective-permute-start(bf16[32,1536]{1,0:T(8,128)(2,1)S(1)} %get-tuple-element.31), channel_id=1, source_target_pairs={{0,64},{64,0},{128,192},{192,128},{1,65},{65,1},{129,193},{193,129... | collective-permute-start | bytes 294920 | tf_op jit(solution)/shard_map/ppermute | solution.py:25
  25.5 0.5 prepare.1
  26.0 0.0 copy-start.1
  26.0 3.5 %collective-permute-start.10 = (bf16[32,1536]{1,0:T(8,128)(2,1)S(1)}, bf16[32,1536]{1,0:T(8,128)(2,1)S(1)}, u32[]{:S(2)}, u32[]{:S(2)}) collective-permute-start(bf16[32,1536]{1,0:T(8,128)(2,1)S(1)} %get-tuple-element.36), channel_id=1, source_target_pairs={{0,192},{64,128},{128,64},{192,0},{1,193},{65,129},{129,65},{193,1... | collective-permute-start | bytes 294920 | tf_op jit(solution)/shard_map/ppermute | solution.py:25
  29.5 0.0 collective-permute-start.11
  29.5 0.0 copy-done
  29.5 0.1 constant_dynamic-slice_fusion.3
  29.6 0.1 shard_map.83.three
  29.8 4.0 %collective-permute-done.10.one = bf16[32,1536]{1,0:T(8,128)(2,1)S(1)} collective-permute-done((bf16[32,1536]{1,0:T(8,128)(2,1)S(1)}, bf16[32,1536]{1,0:T(8,128)(2,1)S(1)}, u32[]{:S(2)}, u32[]{:S(2)}) %collective-permute-start.10) | collective-permute-done | bytes 98336 | tf_op jit(solution)/shard_map/ppermute | solution.py:25
  33.8 1.8 %collective-permute-done.11.two = bf16[32,1536]{1,0:T(8,128)(2,1)S(1)} collective-permute-done((bf16[32,1536]{1,0:T(8,128)(2,1)S(1)}, bf16[32,1536]{1,0:T(8,128)(2,1)S(1)}, u32[]{:S(2)}, u32[]{:S(2)}) %collective-permute-start.11) | collective-permute-done | bytes 98336 | tf_op jit(solution)/shard_map/ppermute | solution.py:25
  35.6 0.0 collective-permute-done.9.mine
  35.6 0.4 aggregate.1
  36.0 3.3 %collective-permute-start.12 = (bf16[32,640]{1,0:T(8,128)(2,1)S(1)}, bf16[32,640]{1,0:T(8,128)(2,1)S(1)}, u32[]{:S(2)}, u32[]{:S(2)}) collective-permute-start(bf16[32,640]{1,0:T(8,128)(2,1)S(1)} %get-tuple-element.42), channel_id=1, source_target_pairs={{0,2},{1,3},{2,0},{3,1},{4,6},{5,7},{6,4},{7,5},{8,10},{9,11},{10,... | collective-permute-start | bytes 122888 | tf_op jit(solution)/shard_map/ppermute | solution.py:25
  39.3 1.1 %collective-permute-start.13 = (bf16[32,640]{1,0:T(8,128)(2,1)S(1)}, bf16[32,640]{1,0:T(8,128)(2,1)S(1)}, u32[]{:S(2)}, u32[]{:S(2)}) collective-permute-start(bf16[32,640]{1,0:T(8,128)(2,1)S(1)} %get-tuple-element.43), channel_id=1, source_target_pairs={{0,3},{1,2},{2,1},{3,0},{4,7},{5,6},{6,5},{7,4},{8,11},{9,10},{10,... | collective-permute-start | bytes 122888 | tf_op jit(solution)/shard_map/ppermute | solution.py:25
  40.4 0.0 collective-permute-start.14
  40.4 0.0 copy-done.1
  40.4 0.1 copy.9.bias
  40.5 1.3 %collective-permute-done.12.two = bf16[32,640]{1,0:T(8,128)(2,1)S(1)} collective-permute-done((bf16[32,640]{1,0:T(8,128)(2,1)S(1)}, bf16[32,640]{1,0:T(8,128)(2,1)S(1)}, u32[]{:S(2)}, u32[]{:S(2)}) %collective-permute-start.12) | collective-permute-done | bytes 40992 | tf_op jit(solution)/shard_map/ppermute | solution.py:25
  41.7 2.8 %collective-permute-done.13.three = bf16[32,640]{1,0:T(8,128)(2,1)S(1)} collective-permute-done((bf16[32,640]{1,0:T(8,128)(2,1)S(1)}, bf16[32,640]{1,0:T(8,128)(2,1)S(1)}, u32[]{:S(2)}, u32[]{:S(2)}) %collective-permute-start.13) | collective-permute-done | bytes 40992 | tf_op jit(solution)/shard_map/ppermute | solution.py:25
  44.5 0.2 mix.1.begun
  44.8 0.0 collective-permute-done.14.part
  44.8 0.8 %finish.1 = bf16[64,512]{1,0:T(8,128)(2,1)} custom-call(f32[64,512]{1,0:T(8,128)S(1)} %mix.1.begun, bf16[32,640]{1,0:T(8,128)(2,1)S(1)} %collective-permute-done.14.part), custom_call_target="tpu_custom_call" | custom-call | tf_op jit(solution)/shard_map/finish/pallas_call | solution.py:309
  (10 shorter events, 0.1 us)
Async XLA Ops:
  2.5 27.0 %copy-start = (bf16[32,256]{1,0:T(8,128)(2,1)S(1)}, bf16[32,256]{1,0:T(8,128)(2,1)}, u32[]{:S(2)}) copy-start(bf16[32,256]{1,0:T(8,128)(2,1)} %param.9) | copy-start | bytes 49156
  2.6 1.3 %collective-permute-start.1 = (bf16[32,512]{1,0:T(8,128)(2,1)S(1)}, bf16[32,512]{1,0:T(8,128)(2,1)S(1)}, u32[]{:S(2)}, u32[]{:S(2)}) collective-permute-start(bf16[32,512]{1,0:T(8,128)(2,1)S(1)} %get-tuple-element.28.refs_0_.refs_2_.scaled.refs_1_), channel_id=1, source_target_pairs={{0,4},{4,0},{1,5},{5,1},{2,6},{6,2},{3,7},{7,3},{8,12},{12,8},{9,1... | collective-permute-start | bytes 98312 | tf_op jit(solution)/shard_map/ppermute | solution.py:21
  3.9 8.7 %collective-permute-start.2 = (bf16[64,512]{1,0:T(8,128)(2,1)S(1)}, bf16[64,512]{1,0:T(8,128)(2,1)S(1)}, u32[]{:S(2)}, u32[]{:S(2)}) collective-permute-start(bf16[64,512]{1,0:T(8,128)(2,1)S(1)} %join.2.refs_0_), channel_id=1, source_target_pairs={{0,16},{4,52},{8,24},{12,60},{16,32},{20,4},{24,40},{28,12},{32,48... | collective-permute-start | bytes 196616 | tf_op jit(solution)/shard_map/ppermute | solution.py:31
  6.8 11.2 %collective-permute-start = (s32[8,256]{1,0:T(8,128)S(1)}, s32[8,256]{1,0:T(8,128)S(1)}, u32[]{:S(2)}, u32[]{:S(2)}) collective-permute-start(s32[8,256]{1,0:T(8,128)S(1)} %get-tuple-element.29.refs_0_), channel_id=1, source_target_pairs={{0,64},{64,0},{128,192},{192,128},{1,65},{65,1},{129,193},{193,129... | collective-permute-start | bytes 24584 | tf_op jit(solution)/shard_map/ppermute | solution.py:25
  12.6 9.6 %collective-permute-start.4 = (bf16[128,512]{1,0:T(8,128)(2,1)S(1)}, bf16[128,512]{1,0:T(8,128)(2,1)S(1)}, u32[]{:S(2)}, u32[]{:S(2)}) collective-permute-start(bf16[128,512]{1,0:T(8,128)(2,1)S(1)} %join.3), channel_id=1, source_target_pairs={{0,8},{4,60},{8,16},{12,4},{16,24},{20,12},{24,32},{28,20},{32,40}... | collective-permute-start | bytes 393224 | tf_op jit(solution)/shard_map/ppermute | solution.py:31
  13.0 8.7 %collective-permute-start.5 = (bf16[32,512]{1,0:T(8,128)(2,1)S(1)}, bf16[32,512]{1,0:T(8,128)(2,1)S(1)}, u32[]{:S(2)}, u32[]{:S(2)}) collective-permute-start(bf16[32,512]{1,0:T(8,128)(2,1)S(1)} %get-tuple-element.28.refs_0_.refs_2_.scaled.refs_1_), channel_id=1, source_target_pairs={{0,32},{8,40},{16,48},{24,56},{32,0},{40,8},{48,16},{56,24},{1,33}... | collective-permute-start | bytes 98312 | tf_op jit(solution)/shard_map/ppermute | solution.py:21
  18.0 4.3 %collective-permute-start.3 = (s32[16,256]{1,0:T(8,128)S(1)}, s32[16,256]{1,0:T(8,128)S(1)}, u32[]{:S(2)}, u32[]{:S(2)}) collective-permute-start(s32[16,256]{1,0:T(8,128)S(1)} %pad_add_fusion), channel_id=1, source_target_pairs={{0,192},{64,128},{128,64},{192,0},{1,193},{65,129},{129,65},{193,1... | collective-permute-start | bytes 49160 | tf_op jit(solution)/shard_map/ppermute | solution.py:25
  21.7 1.2 %collective-permute-start.8 = (bf16[32,512]{1,0:T(8,128)(2,1)S(1)}, bf16[32,512]{1,0:T(8,128)(2,1)S(1)}, u32[]{:S(2)}, u32[]{:S(2)}) collective-permute-start(bf16[32,512]{1,0:T(8,128)(2,1)S(1)} %collective-permute-done.5.refs_6_.refs_5_), channel_id=1, source_target_pairs={{0,4},{4,0},{1,5},{5,1},{2,6},{6,2},{3,7},{7,3},{8,12},{12,8},{9,1... | collective-permute-start | bytes 98312 | tf_op jit(solution)/shard_map/ppermute | solution.py:21
  21.8 1.3 %collective-permute-start.6 = (bf16[64,512]{1,0:T(8,128)(2,1)S(1)}, bf16[64,512]{1,0:T(8,128)(2,1)S(1)}, u32[]{:S(2)}, u32[]{:S(2)}) collective-permute-start(bf16[64,512]{1,0:T(8,128)(2,1)S(1)} %collective-permute-done.2.refs_1_.refs_4_.refs_3_), channel_id=1, source_target_pairs={{0,4},{4,0},{1,5},{5,1},{2,6},{6,2},{3,7},{7,3},{8,12},{12,8},{9,1... | collective-permute-start | bytes 196616 | tf_op jit(solution)/shard_map/ppermute | solution.py:21
  22.2 1.3 %collective-permute-start.7 = (bf16[128,512]{1,0:T(8,128)(2,1)S(1)}, bf16[128,512]{1,0:T(8,128)(2,1)S(1)}, u32[]{:S(2)}, u32[]{:S(2)}) collective-permute-start(bf16[128,512]{1,0:T(8,128)(2,1)S(1)} %collective-permute-done.4.refs_5_.refs_4_), channel_id=1, source_target_pairs={{0,4},{4,0},{1,5},{5,1},{2,6},{6,2},{3,7},{7,3},{8,12},{12,8},{9,1... | collective-permute-start | bytes 393224 | tf_op jit(solution)/shard_map/ppermute | solution.py:21
  24.0 11.6 %collective-permute-start.9 = (bf16[32,1536]{1,0:T(8,128)(2,1)S(1)}, bf16[32,1536]{1,0:T(8,128)(2,1)S(1)}, u32[]{:S(2)}, u32[]{:S(2)}) collective-permute-start(bf16[32,1536]{1,0:T(8,128)(2,1)S(1)} %get-tuple-element.31), channel_id=1, source_target_pairs={{0,64},{64,0},{128,192},{192,128},{1,65},{65,1},{129,193},{193,129... | collective-permute-start | bytes 294920 | tf_op jit(solution)/shard_map/ppermute | solution.py:25
  26.0 14.4 %copy-start.1 = (f32[64]{0:T(128)S(1)}, f32[64]{0:T(128)}, u32[]{:S(2)}) copy-start(f32[64]{0:T(128)} %param.10) | copy-start | bytes 772
  26.0 7.8 %collective-permute-start.10 = (bf16[32,1536]{1,0:T(8,128)(2,1)S(1)}, bf16[32,1536]{1,0:T(8,128)(2,1)S(1)}, u32[]{:S(2)}, u32[]{:S(2)}) collective-permute-start(bf16[32,1536]{1,0:T(8,128)(2,1)S(1)} %get-tuple-element.36), channel_id=1, source_target_pairs={{0,192},{64,128},{128,64},{192,0},{1,193},{65,129},{129,65},{193,1... | collective-permute-start | bytes 294920 | tf_op jit(solution)/shard_map/ppermute | solution.py:25
  29.5 6.1 %collective-permute-start.11 = (bf16[32,1536]{1,0:T(8,128)(2,1)S(1)}, bf16[32,1536]{1,0:T(8,128)(2,1)S(1)}, u32[]{:S(2)}, u32[]{:S(2)}) collective-permute-start(bf16[32,1536]{1,0:T(8,128)(2,1)S(1)} %get-tuple-element.37), channel_id=1, source_target_pairs={{0,128},{64,192},{128,0},{192,64},{1,129},{65,193},{129,1},{193,65... | collective-permute-start | bytes 294920 | tf_op jit(solution)/shard_map/ppermute | solution.py:25
  36.0 5.7 %collective-permute-start.12 = (bf16[32,640]{1,0:T(8,128)(2,1)S(1)}, bf16[32,640]{1,0:T(8,128)(2,1)S(1)}, u32[]{:S(2)}, u32[]{:S(2)}) collective-permute-start(bf16[32,640]{1,0:T(8,128)(2,1)S(1)} %get-tuple-element.42), channel_id=1, source_target_pairs={{0,2},{1,3},{2,0},{3,1},{4,6},{5,7},{6,4},{7,5},{8,10},{9,11},{10,... | collective-permute-start | bytes 122888 | tf_op jit(solution)/shard_map/ppermute | solution.py:25
  39.3 5.2 %collective-permute-start.13 = (bf16[32,640]{1,0:T(8,128)(2,1)S(1)}, bf16[32,640]{1,0:T(8,128)(2,1)S(1)}, u32[]{:S(2)}, u32[]{:S(2)}) collective-permute-start(bf16[32,640]{1,0:T(8,128)(2,1)S(1)} %get-tuple-element.43), channel_id=1, source_target_pairs={{0,3},{1,2},{2,1},{3,0},{4,7},{5,6},{6,5},{7,4},{8,11},{9,10},{10,... | collective-permute-start | bytes 122888 | tf_op jit(solution)/shard_map/ppermute | solution.py:25
  40.4 4.4 %collective-permute-start.14 = (bf16[32,640]{1,0:T(8,128)(2,1)S(1)}, bf16[32,640]{1,0:T(8,128)(2,1)S(1)}, u32[]{:S(2)}, u32[]{:S(2)}) collective-permute-start(bf16[32,640]{1,0:T(8,128)(2,1)S(1)} %get-tuple-element.44), channel_id=1, source_target_pairs={{0,1},{1,0},{2,3},{3,2},{4,5},{5,4},{6,7},{7,6},{8,9},{9,8},{10,11... | collective-permute-start | bytes 122888 | tf_op jit(solution)/shard_map/ppermute | solution.py:25

commit v4 on v3

--- a/solution.py
+++ b/solution.py
@@ -188,7 +188,7 @@
     at = 0
     for piece in pieces:
         for k in range(piece.shape[0] // FEATS):
-            held[at] = piece[k * FEATS : (k + 1) * FEATS, :].astype(jnp.float32)
+            held[at] = piece[k * FEATS : (k + 1) * FEATS, :]
             at += 1
     for dest, (request, top), out in zip(dests, requests, outs):
         out[...] = jnp.zeros_like(out)
@@ -204,7 +204,7 @@
                     block = rows >> 7
                     picked = jnp.zeros((FEATS, LANES), jnp.float32)
                     for t in range(4):
-                        part = held[which, :, t * LANES : (t + 1) * LANES]
+                        part = held[which, :, t * LANES : (t + 1) * LANES].astype(jnp.float32)
                         took = jnp.take_along_axis(part, lane, axis=1, mode="promise_in_bounds")
                         picked = jnp.where(block == t, took, picked)
                     to = s * 256 + g * LANES
@@ -218,7 +218,7 @@
         out_shape=[VMEM((FEATS, 1536), jnp.bfloat16)] * len(dests),
         in_specs=[pl.BlockSpec(memory_space=pltpu.SMEM)] + whole(len(operands)),
         out_specs=whole(len(dests)),
-        scratch_shapes=[VMEM((16, FEATS, 512), jnp.float32)],
+        scratch_shapes=[VMEM((16, FEATS, 512), jnp.bfloat16)],
         compiler_params=pltpu.CompilerParams(vmem_limit_bytes=8 * 2**20),
     )(pltpu.with_memory_space_constraint(table, pltpu.SMEM), *operands)
 
@@ -326,7 +326,7 @@
     same = (wanted & 1) == my_core
     place = jnp.zeros_like(wanted)
     for distance, (ours, theirs) in enumerate(
-        ((0, 1), (4, 5), (2, 3), (6, 7), (8, 15), (14, 13), (10, 9), (12, 11))
+        ((0, 1), (4, 5), (2, 3), (6, 7), (8, 11), (15, 14), (10, 9), (13, 12))
     ):
         place = jnp.where(ahead == distance, jnp.where(same, ours, theirs), place)
     here = (wanted >= 0) & ((wanted >> 4) == my_x)
@@ -346,7 +346,7 @@
     across = paired(jnp.concatenate([late_request, late_beside], axis=0), "x", 3)
     table = piece_table(request, beside, across)
     rest = []
-    for piece in (two, one, four):
+    for piece in (joined(two, four), one):
         rest.append(shifted(piece, "core", 1))
     table = placed(table)
     pieces = (scaled, partner, two, one, four, *rest)

time: 45.7 us -> 45.4 us (level)
    ppermute x5 -> x4, waiting for transfers between devices: 3.93 us -> 3.68 us  [shifted(): lax.ppermute(array, axis, [(i, (i + by) % count) for i in range(count)])]
    ppermute x5 -> x4, starting transfers between devices: 5.73 us -> 5.71 us  [shifted(): lax.ppermute(array, axis, [(i, (i + by) % count) for i in range(count)])]
  transfers between devices with their start and end apart: 15 -> 14, of which waited for: 9 -> 9; matrix products, arithmetic and copies ran while one was open for 1% -> 1% of each run, Pallas kernels for 3% -> 3%
where the time goes in v4:
time: 45.4 us; the launch traced here: 45.3 us
  starting transfers between devices  20.4 us (45%)
  waiting for transfers between devices  19 us (42%)
  Pallas kernels  5.56 us (12%)
    ppermute x8, starting transfers between devices, paired(): lax.ppermute(array, axis, [(i, i ^ by) for i in range(lax.axis_size(axis))])  11.3 us
    ppermute x8, waiting for transfers between devices, paired(): lax.ppermute(array, axis, [(i, i ^ by) for i in range(lax.axis_size(axis))])  9.94 us
    ppermute x4, starting transfers between devices, shifted(): lax.ppermute(array, axis, [(i, (i + by) % count) for i in range(count)])  5.71 us
    ppermute x2, waiting for transfers between devices, opposed(): return lax.ppermute(array, ('z', 'core'), pairs)  5.35 us
    ppermute x4, waiting for transfers between devices, shifted(): lax.ppermute(array, axis, [(i, (i + by) % count) for i in range(count)])  3.68 us
    ppermute x2, starting transfers between devices, opposed(): return lax.ppermute(array, ('z', 'core'), pairs)  3.33 us
    pallas_call x1, Pallas kernels, head(): pl.pallas_call(head_kernel, out_shape=[VMEM((FEATS, 512), jnp.bfloat16),...  2.54 us
  transfers between devices with their start and end apart: 14, of which 9 were waited for; matrix products, arithmetic and copies ran while one was open for 1% of the time, Pallas kernels for 3%

profile of v4, /device:TPU:2, one launch (start us, length us, event | category | flops | bytes accessed | tf_op | source)
XLA Modules:
  0.0 45.3 jit_solution(3398117503595562943)
XLA Ops:
  0.0 2.5 %head.1 = (bf16[32,512]{1,0:T(8,128)(2,1)S(1)}, f32[1,512]{1,0:T(1,128)S(1)}, s32[8,256]{1,0:T(8,128)S(1)}, bf16[512,512]{1,0:T(8,128)(2,1)S(1)}, bf16[6,512,256]{2,1,0:T(8,128)(2,1)S(1)}) custom-call(s32[1,6]{1,0:T(1,128)} %sources_in.1, s32[1,512,512]{2,1,0:T(8,128)} %self_in.1, s32[1,6,512,256]{3,2,1,0:T(8,128)} %halo_in.1, s32[1,512]{1,0:T(1,128)} %bitcast.12, ...), custom_call_target="tpu_custom_call" | custom-call | tf_op jit(solution)/shard_map/head/pallas_call | solution.py:124
  2.5 0.1 collective-permute-start.1
  2.6 1.2 %collective-permute-done.1.refs_1_.refs_3_.refs_2_ = bf16[32,512]{1,0:T(8,128)(2,1)S(1)} collective-permute-done((bf16[32,512]{1,0:T(8,128)(2,1)S(1)}, bf16[32,512]{1,0:T(8,128)(2,1)S(1)}, u32[]{:S(2)}, u32[]{:S(2)}) %collective-permute-start.1) | collective-permute-done | bytes 32800 | tf_op jit(solution)/shard_map/ppermute | solution.py:21
  3.8 2.9 %collective-permute-start.2 = (bf16[64,512]{1,0:T(8,128)(2,1)S(1)}, bf16[64,512]{1,0:T(8,128)(2,1)S(1)}, u32[]{:S(2)}, u32[]{:S(2)}) collective-permute-start(bf16[64,512]{1,0:T(8,128)(2,1)S(1)} %join.3.refs_0_), channel_id=1, source_target_pairs={{0,16},{4,52},{8,24},{12,60},{16,32},{20,4},{24,40},{28,12},{32,48... | collective-permute-start | bytes 196616 | tf_op jit(solution)/shard_map/ppermute | solution.py:31
  6.8 0.0 copy-start
  6.8 0.4 collective-permute-start
  7.2 5.3 %collective-permute-done.2.refs_1_.refs_0_.refs_4_.refs_3_ = bf16[64,512]{1,0:T(8,128)(2,1)S(1)} collective-permute-done((bf16[64,512]{1,0:T(8,128)(2,1)S(1)}, bf16[64,512]{1,0:T(8,128)(2,1)S(1)}, u32[]{:S(2)}, u32[]{:S(2)}) %collective-permute-start.2) | collective-permute-done | bytes 65568 | tf_op jit(solution)/shard_map/ppermute | solution.py:31
  12.6 0.4 collective-permute-start.4
  13.0 5.0 %collective-permute-start.5 = (bf16[32,512]{1,0:T(8,128)(2,1)S(1)}, bf16[32,512]{1,0:T(8,128)(2,1)S(1)}, u32[]{:S(2)}, u32[]{:S(2)}) collective-permute-start(bf16[32,512]{1,0:T(8,128)(2,1)S(1)} %get-tuple-element.28.refs_0_.refs_2_.scaled.refs_1_), channel_id=1, source_target_pairs={{0,32},{8,40},{16,48},{24,56},{32,0},{40,8},{48,16},{56,24},{1,33}... | collective-permute-start | bytes 98312 | tf_op jit(solution)/shard_map/ppermute | solution.py:21
  18.0 0.0 collective-permute-done.refs_0_
  18.0 1.5 %collective-permute-start.3 = (s32[16,256]{1,0:T(8,128)S(1)}, s32[16,256]{1,0:T(8,128)S(1)}, u32[]{:S(2)}, u32[]{:S(2)}) collective-permute-start(s32[16,256]{1,0:T(8,128)S(1)} %pad_add_fusion), channel_id=1, source_target_pairs={{0,192},{64,128},{128,64},{192,0},{1,193},{65,129},{129,65},{193,1... | collective-permute-start | bytes 49160 | tf_op jit(solution)/shard_map/ppermute | solution.py:25
  19.5 2.1 %collective-permute-done.5.refs_1_.refs_6_.refs_5_ = bf16[32,512]{1,0:T(8,128)(2,1)S(1)} collective-permute-done((bf16[32,512]{1,0:T(8,128)(2,1)S(1)}, bf16[32,512]{1,0:T(8,128)(2,1)S(1)}, u32[]{:S(2)}, u32[]{:S(2)}) %collective-permute-start.5) | collective-permute-done | bytes 32800 | tf_op jit(solution)/shard_map/ppermute | solution.py:21
  21.7 0.2 collective-permute-start.6
  21.8 0.0 collective-permute-done.4.refs_5_.refs_4_
  21.9 0.4 collective-permute-start.7
  22.3 0.0 collective-permute-done.3.refs_1_
  22.3 0.6 %place.1.table = s32[4,128]{1,0:T(4,128)S(4)} custom-call(s32[4,128]{1,0:T(4,128)S(1)} %select_select_fusion.listed), custom_call_target="tpu_custom_call" | custom-call | tf_op jit(solution)/shard_map/place/pallas_call | solution.py:171
  22.9 0.2 collective-permute-done.6.refs_7_.refs_6_
  23.0 0.2 collective-permute-done.7.refs_8_.refs_7_
  23.2 0.4 shard_map.82
  23.7 1.8 %collective-permute-start.8 = (bf16[32,1536]{1,0:T(8,128)(2,1)S(1)}, bf16[32,1536]{1,0:T(8,128)(2,1)S(1)}, u32[]{:S(2)}, u32[]{:S(2)}) collective-permute-start(bf16[32,1536]{1,0:T(8,128)(2,1)S(1)} %get-tuple-element.31), channel_id=1, source_target_pairs={{0,64},{64,0},{128,192},{192,128},{1,65},{65,1},{129,193},{193,129... | collective-permute-start | bytes 294920 | tf_op jit(solution)/shard_map/ppermute | solution.py:25
  25.5 0.5 prepare.1
  25.9 0.0 copy-start.1
  26.0 3.2 %collective-permute-start.9 = (bf16[32,1536]{1,0:T(8,128)(2,1)S(1)}, bf16[32,1536]{1,0:T(8,128)(2,1)S(1)}, u32[]{:S(2)}, u32[]{:S(2)}) collective-permute-start(bf16[32,1536]{1,0:T(8,128)(2,1)S(1)} %get-tuple-element.36), channel_id=1, source_target_pairs={{0,192},{64,128},{128,64},{192,0},{1,193},{65,129},{129,65},{193,1... | collective-permute-start | bytes 294920 | tf_op jit(solution)/shard_map/ppermute | solution.py:25
  29.2 0.0 collective-permute-start.10
  29.2 0.0 copy-done
  29.2 0.1 constant_dynamic-slice_fusion.3
  29.3 0.1 shard_map.83.three
  29.4 4.0 %collective-permute-done.9.one = bf16[32,1536]{1,0:T(8,128)(2,1)S(1)} collective-permute-done((bf16[32,1536]{1,0:T(8,128)(2,1)S(1)}, bf16[32,1536]{1,0:T(8,128)(2,1)S(1)}, u32[]{:S(2)}, u32[]{:S(2)}) %collective-permute-start.9) | collective-permute-done | bytes 98336 | tf_op jit(solution)/shard_map/ppermute | solution.py:25
  33.5 1.8 %collective-permute-done.10.two = bf16[32,1536]{1,0:T(8,128)(2,1)S(1)} collective-permute-done((bf16[32,1536]{1,0:T(8,128)(2,1)S(1)}, bf16[32,1536]{1,0:T(8,128)(2,1)S(1)}, u32[]{:S(2)}, u32[]{:S(2)}) %collective-permute-start.10) | collective-permute-done | bytes 98336 | tf_op jit(solution)/shard_map/ppermute | solution.py:25
  35.3 0.0 collective-permute-done.8.mine
  35.3 0.4 aggregate.1
  35.7 3.3 %collective-permute-start.11 = (bf16[32,640]{1,0:T(8,128)(2,1)S(1)}, bf16[32,640]{1,0:T(8,128)(2,1)S(1)}, u32[]{:S(2)}, u32[]{:S(2)}) collective-permute-start(bf16[32,640]{1,0:T(8,128)(2,1)S(1)} %get-tuple-element.42), channel_id=1, source_target_pairs={{0,2},{1,3},{2,0},{3,1},{4,6},{5,7},{6,4},{7,5},{8,10},{9,11},{10,... | collective-permute-start | bytes 122888 | tf_op jit(solution)/shard_map/ppermute | solution.py:25
  39.0 1.1 %collective-permute-start.12 = (bf16[32,640]{1,0:T(8,128)(2,1)S(1)}, bf16[32,640]{1,0:T(8,128)(2,1)S(1)}, u32[]{:S(2)}, u32[]{:S(2)}) collective-permute-start(bf16[32,640]{1,0:T(8,128)(2,1)S(1)} %get-tuple-element.43), channel_id=1, source_target_pairs={{0,3},{1,2},{2,1},{3,0},{4,7},{5,6},{6,5},{7,4},{8,11},{9,10},{10,... | collective-permute-start | bytes 122888 | tf_op jit(solution)/shard_map/ppermute | solution.py:25
  40.0 0.0 collective-permute-start.13
  40.0 0.0 copy-done.1
  40.0 0.1 copy.9.bias
  40.1 1.2 %collective-permute-done.11.two = bf16[32,640]{1,0:T(8,128)(2,1)S(1)} collective-permute-done((bf16[32,640]{1,0:T(8,128)(2,1)S(1)}, bf16[32,640]{1,0:T(8,128)(2,1)S(1)}, u32[]{:S(2)}, u32[]{:S(2)}) %collective-permute-start.11) | collective-permute-done | bytes 40992 | tf_op jit(solution)/shard_map/ppermute | solution.py:25
  41.3 2.9 %collective-permute-done.12.three = bf16[32,640]{1,0:T(8,128)(2,1)S(1)} collective-permute-done((bf16[32,640]{1,0:T(8,128)(2,1)S(1)}, bf16[32,640]{1,0:T(8,128)(2,1)S(1)}, u32[]{:S(2)}, u32[]{:S(2)}) %collective-permute-start.12) | collective-permute-done | bytes 40992 | tf_op jit(solution)/shard_map/ppermute | solution.py:25
  44.2 0.2 mix.1.begun
  44.4 0.0 collective-permute-done.13.part
  44.5 0.8 %finish.1 = bf16[64,512]{1,0:T(8,128)(2,1)} custom-call(f32[64,512]{1,0:T(8,128)S(1)} %mix.1.begun, bf16[32,640]{1,0:T(8,128)(2,1)S(1)} %collective-permute-done.13.part), custom_call_target="tpu_custom_call" | custom-call | tf_op jit(solution)/shard_map/finish/pallas_call | solution.py:309
  (11 shorter events, 0.1 us)
Async XLA Ops:
  2.5 1.3 %collective-permute-start.1 = (bf16[32,512]{1,0:T(8,128)(2,1)S(1)}, bf16[32,512]{1,0:T(8,128)(2,1)S(1)}, u32[]{:S(2)}, u32[]{:S(2)}) collective-permute-start(bf16[32,512]{1,0:T(8,128)(2,1)S(1)} %get-tuple-element.28.refs_0_.refs_2_.scaled.refs_1_), channel_id=1, source_target_pairs={{0,4},{4,0},{1,5},{5,1},{2,6},{6,2},{3,7},{7,3},{8,12},{12,8},{9,1... | collective-permute-start | bytes 98312 | tf_op jit(solution)/shard_map/ppermute | solution.py:21
  3.8 8.7 %collective-permute-start.2 = (bf16[64,512]{1,0:T(8,128)(2,1)S(1)}, bf16[64,512]{1,0:T(8,128)(2,1)S(1)}, u32[]{:S(2)}, u32[]{:S(2)}) collective-permute-start(bf16[64,512]{1,0:T(8,128)(2,1)S(1)} %join.3.refs_0_), channel_id=1, source_target_pairs={{0,16},{4,52},{8,24},{12,60},{16,32},{20,4},{24,40},{28,12},{32,48... | collective-permute-start | bytes 196616 | tf_op jit(solution)/shard_map/ppermute | solution.py:31
  6.8 22.4 %copy-start = (bf16[32,256]{1,0:T(8,128)(2,1)S(1)}, bf16[32,256]{1,0:T(8,128)(2,1)}, u32[]{:S(2)}) copy-start(bf16[32,256]{1,0:T(8,128)(2,1)} %param.9) | copy-start | bytes 49156
  6.8 11.2 %collective-permute-start = (s32[8,256]{1,0:T(8,128)S(1)}, s32[8,256]{1,0:T(8,128)S(1)}, u32[]{:S(2)}, u32[]{:S(2)}) collective-permute-start(s32[8,256]{1,0:T(8,128)S(1)} %get-tuple-element.29.refs_0_), channel_id=1, source_target_pairs={{0,64},{64,0},{128,192},{192,128},{1,65},{65,1},{129,193},{193,129... | collective-permute-start | bytes 24584 | tf_op jit(solution)/shard_map/ppermute | solution.py:25
  12.6 9.3 %collective-permute-start.4 = (bf16[128,512]{1,0:T(8,128)(2,1)S(1)}, bf16[128,512]{1,0:T(8,128)(2,1)S(1)}, u32[]{:S(2)}, u32[]{:S(2)}) collective-permute-start(bf16[128,512]{1,0:T(8,128)(2,1)S(1)} %join.4), channel_id=1, source_target_pairs={{0,8},{4,60},{8,16},{12,4},{16,24},{20,12},{24,32},{28,20},{32,40}... | collective-permute-start | bytes 393224 | tf_op jit(solution)/shard_map/ppermute | solution.py:31
  13.0 8.7 %collective-permute-start.5 = (bf16[32,512]{1,0:T(8,128)(2,1)S(1)}, bf16[32,512]{1,0:T(8,128)(2,1)S(1)}, u32[]{:S(2)}, u32[]{:S(2)}) collective-permute-start(bf16[32,512]{1,0:T(8,128)(2,1)S(1)} %get-tuple-element.28.refs_0_.refs_2_.scaled.refs_1_), channel_id=1, source_target_pairs={{0,32},{8,40},{16,48},{24,56},{32,0},{40,8},{48,16},{56,24},{1,33}... | collective-permute-start | bytes 98312 | tf_op jit(solution)/shard_map/ppermute | solution.py:21
  18.0 4.3 %collective-permute-start.3 = (s32[16,256]{1,0:T(8,128)S(1)}, s32[16,256]{1,0:T(8,128)S(1)}, u32[]{:S(2)}, u32[]{:S(2)}) collective-permute-start(s32[16,256]{1,0:T(8,128)S(1)} %pad_add_fusion), channel_id=1, source_target_pairs={{0,192},{64,128},{128,64},{192,0},{1,193},{65,129},{129,65},{193,1... | collective-permute-start | bytes 49160 | tf_op jit(solution)/shard_map/ppermute | solution.py:25
  21.7 1.4 %collective-permute-start.6 = (bf16[96,512]{1,0:T(8,128)(2,1)S(1)}, bf16[96,512]{1,0:T(8,128)(2,1)S(1)}, u32[]{:S(2)}, u32[]{:S(2)}) collective-permute-start(bf16[96,512]{1,0:T(8,128)(2,1)S(1)} %join.5), channel_id=1, source_target_pairs={{0,4},{4,0},{1,5},{5,1},{2,6},{6,2},{3,7},{7,3},{8,12},{12,8},{9,1... | collective-permute-start | bytes 294920 | tf_op jit(solution)/shard_map/ppermute | solution.py:21
  21.9 1.4 %collective-permute-start.7 = (bf16[128,512]{1,0:T(8,128)(2,1)S(1)}, bf16[128,512]{1,0:T(8,128)(2,1)S(1)}, u32[]{:S(2)}, u32[]{:S(2)}) collective-permute-start(bf16[128,512]{1,0:T(8,128)(2,1)S(1)} %collective-permute-done.4.refs_5_.refs_4_), channel_id=1, source_target_pairs={{0,4},{4,0},{1,5},{5,1},{2,6},{6,2},{3,7},{7,3},{8,12},{12,8},{9,1... | collective-permute-start | bytes 393224 | tf_op jit(solution)/shard_map/ppermute | solution.py:21
  23.7 11.6 %collective-permute-start.8 = (bf16[32,1536]{1,0:T(8,128)(2,1)S(1)}, bf16[32,1536]{1,0:T(8,128)(2,1)S(1)}, u32[]{:S(2)}, u32[]{:S(2)}) collective-permute-start(bf16[32,1536]{1,0:T(8,128)(2,1)S(1)} %get-tuple-element.31), channel_id=1, source_target_pairs={{0,64},{64,0},{128,192},{192,128},{1,65},{65,1},{129,193},{193,129... | collective-permute-start | bytes 294920 | tf_op jit(solution)/shard_map/ppermute | solution.py:25
  25.9 14.1 %copy-start.1 = (f32[64]{0:T(128)S(1)}, f32[64]{0:T(128)}, u32[]{:S(2)}) copy-start(f32[64]{0:T(128)} %param.10) | copy-start | bytes 772
  26.0 7.5 %collective-permute-start.9 = (bf16[32,1536]{1,0:T(8,128)(2,1)S(1)}, bf16[32,1536]{1,0:T(8,128)(2,1)S(1)}, u32[]{:S(2)}, u32[]{:S(2)}) collective-permute-start(bf16[32,1536]{1,0:T(8,128)(2,1)S(1)} %get-tuple-element.36), channel_id=1, source_target_pairs={{0,192},{64,128},{128,64},{192,0},{1,193},{65,129},{129,65},{193,1... | collective-permute-start | bytes 294920 | tf_op jit(solution)/shard_map/ppermute | solution.py:25
  29.2 6.1 %collective-permute-start.10 = (bf16[32,1536]{1,0:T(8,128)(2,1)S(1)}, bf16[32,1536]{1,0:T(8,128)(2,1)S(1)}, u32[]{:S(2)}, u32[]{:S(2)}) collective-permute-start(bf16[32,1536]{1,0:T(8,128)(2,1)S(1)} %get-tuple-element.37), channel_id=1, source_target_pairs={{0,128},{64,192},{128,0},{192,64},{1,129},{65,193},{129,1},{193,65... | collective-permute-start | bytes 294920 | tf_op jit(solution)/shard_map/ppermute | solution.py:25
  35.7 5.6 %collective-permute-start.11 = (bf16[32,640]{1,0:T(8,128)(2,1)S(1)}, bf16[32,640]{1,0:T(8,128)(2,1)S(1)}, u32[]{:S(2)}, u32[]{:S(2)}) collective-permute-start(bf16[32,640]{1,0:T(8,128)(2,1)S(1)} %get-tuple-element.42), channel_id=1, source_target_pairs={{0,2},{1,3},{2,0},{3,1},{4,6},{5,7},{6,4},{7,5},{8,10},{9,11},{10,... | collective-permute-start | bytes 122888 | tf_op jit(solution)/shard_map/ppermute | solution.py:25
  39.0 5.2 %collective-permute-start.12 = (bf16[32,640]{1,0:T(8,128)(2,1)S(1)}, bf16[32,640]{1,0:T(8,128)(2,1)S(1)}, u32[]{:S(2)}, u32[]{:S(2)}) collective-permute-start(bf16[32,640]{1,0:T(8,128)(2,1)S(1)} %get-tuple-element.43), channel_id=1, source_target_pairs={{0,3},{1,2},{2,1},{3,0},{4,7},{5,6},{6,5},{7,4},{8,11},{9,10},{10,... | collective-permute-start | bytes 122888 | tf_op jit(solution)/shard_map/ppermute | solution.py:25
  40.0 4.4 %collective-permute-start.13 = (bf16[32,640]{1,0:T(8,128)(2,1)S(1)}, bf16[32,640]{1,0:T(8,128)(2,1)S(1)}, u32[]{:S(2)}, u32[]{:S(2)}) collective-permute-start(bf16[32,640]{1,0:T(8,128)(2,1)S(1)} %get-tuple-element.44), channel_id=1, source_target_pairs={{0,1},{1,0},{2,3},{3,2},{4,5},{5,4},{6,7},{7,6},{8,9},{9,8},{10,11... | collective-permute-start | bytes 122888 | tf_op jit(solution)/shard_map/ppermute | solution.py:25
